TPU v7x, 32 devices: a whole 2x2x4 slice. The times are simulated.
32 devices in a mesh: ep: 32 (over z, y, x, core).
Axes of the slice: x: 2, y: 2, z: 4, core: 2. Of those that a mesh axis runs over, the one named last changes fastest.
Arguments:
- hidden: bfloat16 [32768, 1024], P('ep')
- grad_out: bfloat16 [32768, 1024], P('ep')
- w_router: bfloat16 [1024, 32], replicated
- b_router: float32 [32], replicated
- expert_ids: int32 [32768, 8], P('ep')
- slot_ids: int32 [32768, 8], P('ep')
- w_gate_up: bfloat16 [32, 1024, 1024], P('ep')
- b_gate_up: float32 [32, 1024], P('ep')
- w_down: bfloat16 [32, 512, 1024], P('ep')
- b_down: float32 [32, 1024], P('ep')
Outputs:
- output 1: bfloat16 [32768, 1024], P('ep')
- output 2: bfloat16 [32768, 1024], P('ep')
- output 3: float32 [1024, 32], replicated
- output 4: float32 [32], replicated
- output 5: float32 [32, 1024, 1024], P('ep')
- output 6: float32 [32, 1024], P('ep')
- output 7: float32 [32, 512, 1024], P('ep')
- output 8: float32 [32, 1024], P('ep')
All inputs are finite; a program needn't handle non-finite values.
Results may differ from a plain program's by a relative error of at most 0.00975927.
Values are sent between devices in bfloat16 or wider.
A program may use at most 1 GiB of HBM per device.

v0:
```python
import jax
import jax.numpy as jnp
from jax import lax
from jax.sharding import PartitionSpec as P

SWIGLU_LIMIT = 7.0
SWIGLU_ALPHA = 1.702


def swiglu(pre_act):
    col_pairs = pre_act.reshape(pre_act.shape[:-1] + (pre_act.shape[-1] // 2, 2))
    gate_in = jnp.minimum(col_pairs[..., 0], SWIGLU_LIMIT)
    up_in = jnp.clip(col_pairs[..., 1], -SWIGLU_LIMIT, SWIGLU_LIMIT)
    return gate_in * jax.nn.sigmoid(SWIGLU_ALPHA * gate_in) * (up_in + 1.0)


def solution(mesh):
    ep_size = mesh.shape['ep']

    def local_block(hidden, grad_out, w_router, b_router, expert_ids, slot_ids, w_gate_up, b_gate_up, w_down, b_down):
        tok_local, d_model = hidden.shape
        top_k = expert_ids.shape[1]
        experts = w_router.shape[1]
        local_experts = w_gate_up.shape[0]
        capacity = (3 * tok_local * top_k + 2 * experts - 1) // (2 * experts)
        buf_rows = experts * capacity
        copy_count = tok_local * top_k
        dest_row = jnp.where(slot_ids >= 0, expert_ids * capacity + slot_ids, buf_rows)
        src_copy = jnp.full((buf_rows + 1,), copy_count, jnp.int32).at[dest_row.reshape(-1)].set(jnp.arange(copy_count, dtype=jnp.int32))[:buf_rows]
        src_tok = src_copy // top_k
        logits = jnp.dot(hidden, w_router, preferred_element_type=jnp.float32) + b_router
        gate_w = jax.nn.softmax(jnp.take_along_axis(logits, expert_ids, axis=1), axis=-1)

        send_x = jnp.take(hidden, src_tok, axis=0, mode='fill', fill_value=0)
        recv_x = lax.all_to_all(send_x, 'ep', 0, 0, tiled=True).reshape(ep_size, local_experts, capacity, d_model)
        pre_act = jnp.einsum('secd,edf->secf', recv_x, w_gate_up, preferred_element_type=jnp.float32) + b_gate_up[None, :, None, :]
        act_val, act_vjp = jax.vjp(swiglu, pre_act)
        act_bf = act_val.astype(jnp.bfloat16)
        y_rows = (jnp.einsum('secf,efd->secd', act_bf, w_down, preferred_element_type=jnp.float32) + b_down[None, :, None, :]).astype(jnp.bfloat16)
        back_y = lax.all_to_all(y_rows.reshape(buf_rows, d_model), 'ep', 0, 0, tiled=True)
        y_copies = jnp.take(back_y, dest_row, axis=0, mode='fill', fill_value=0)
        block_out = jnp.sum(gate_w[:, :, None] * y_copies, axis=1).astype(jnp.bfloat16)

        gate_grad = jnp.einsum('td,tkd->tk', grad_out, y_copies, preferred_element_type=jnp.float32)
        sel_grad = gate_w * (gate_grad - jnp.sum(gate_w * gate_grad, axis=1, keepdims=True))
        expert_range = jnp.arange(experts, dtype=jnp.int32)
        logit_grad = jnp.sum(jnp.where(expert_ids[:, :, None] == expert_range, sel_grad[:, :, None], 0.0), axis=1).astype(jnp.bfloat16)
        row_gate = jnp.take(gate_w.reshape(-1), src_copy, axis=0, mode='fill', fill_value=0)
        row_grad = jnp.take(grad_out, src_tok, axis=0, mode='fill', fill_value=0)
        send_q = (row_gate[:, None] * row_grad).astype(jnp.bfloat16)
        recv_q = lax.all_to_all(send_q, 'ep', 0, 0, tiled=True).reshape(ep_size, local_experts, capacity, d_model)
        grad_b_down = jnp.sum(recv_q, axis=(0, 2), dtype=jnp.float32)
        grad_w_down = jnp.einsum('secf,secd->efd', act_bf, recv_q, preferred_element_type=jnp.float32)
        act_grad = jnp.einsum('secd,efd->secf', recv_q, w_down, preferred_element_type=jnp.float32)
        pre_grad = act_vjp(act_grad)[0].astype(jnp.bfloat16)
        grad_b_gate_up = jnp.sum(pre_grad, axis=(0, 2), dtype=jnp.float32)
        grad_w_gate_up = jnp.einsum('secd,secf->edf', recv_x, pre_grad, preferred_element_type=jnp.float32)
        p_rows = jnp.einsum('secf,edf->secd', pre_grad, w_gate_up, preferred_element_type=jnp.float32).astype(jnp.bfloat16)
        back_p = lax.all_to_all(p_rows.reshape(buf_rows, d_model), 'ep', 0, 0, tiled=True)
        p_copies = jnp.take(back_p, dest_row, axis=0, mode='fill', fill_value=0)
        router_dx = jnp.einsum('te,de->td', logit_grad, w_router, preferred_element_type=jnp.float32)
        grad_hidden = (jnp.sum(p_copies, axis=1, dtype=jnp.float32) + router_dx).astype(jnp.bfloat16)
        grad_w_router = lax.psum(jnp.einsum('td,te->de', hidden, logit_grad, preferred_element_type=jnp.float32), 'ep')
        grad_b_router = lax.psum(jnp.sum(logit_grad, axis=0, dtype=jnp.float32), 'ep')
        return (block_out, grad_hidden, grad_w_router, grad_b_router, grad_w_gate_up, grad_b_gate_up, grad_w_down, grad_b_down)

    tok_spec = P('ep', None)
    in_specs = (tok_spec, tok_spec, P(None, None), P(None), tok_spec, tok_spec, P('ep', None, None), P('ep', None), P('ep', None, None), P('ep', None))
    out_specs = (tok_spec, tok_spec, P(None, None), P(None), P('ep', None, None), P('ep', None), P('ep', None, None), P('ep', None))
    return jax.shard_map(local_block, mesh=mesh, in_specs=in_specs, out_specs=out_specs, check_vma=False)
```

profile of v0, /device:TPU:0, one launch (start us, length us, event | category | flops | bytes accessed | tf_op | source)
XLA Modules:
  0.0 3078.9 jit_solution(4598818785818094280)
XLA Ops:
  9.3 30.5 scatter_custom_fusion
  40.5 62.4 %gather_fusion.2 = bf16[12288,1024]{1,0:T(8,128)(2,1)} fusion(bf16[1024,1024]{1,0:T(8,128)(2,1)} %param.14, s32[12288]{0:T(1024)S(1)} %get-tuple-element.23), kind=kCustom, calls=%fused_computation.clone | custom fusion | bytes 50380800 | tf_op jit(solution)/shard_map/jit(_take)/gather | solution.py:34
  115.2 565.0 %all_to_all.39 = bf16[32,384,1024]{2,1,0:T(8,128)(2,1)} all-to-all(bf16[32,384,1024]{2,1,0:T(8,128)(2,1)S(1)} %bitcast.167), channel_id=1, replica_groups=mesh['ep'=32] {'ep'}, dimensions={0} | all-to-all | bytes 50331648 | tf_op jit(solution)/shard_map/all_to_all | solution.py:35
  680.3 36.4 %fusion.1 = f32[32,1,384,1024]{3,2,0,1:T(8,128)} fusion(f32[1024]{0:T(1024)S(1)} %bitcast.170, bf16[32,384,1024]{2,1,0:T(8,128)(2,1)} %all_to_all.39, bf16[1,1024,1024]{2,1,0:T(8,128)(2,1)S(1)} %copy-done), kind=kOutput, calls=%fused_computation.10 | convolution fusion | flops 25782386688 | bytes 77598720 | tf_op jit(solution)/shard_map/secd,edf->secf/dot_general | solution.py:36
  716.7 49.5 %copy.91 = f32[32,1,384,1024]{2,0,3,1:T(8,128)} copy(f32[32,1,384,1024]{3,2,0,1:T(8,128)} %fusion.1) | data formatting | bytes 100663296 | tf_op jit(solution)/shard_map/add | solution.py:36
  766.2 32.4 %fusion.56 = (f32[32,1,384,512,1]{2,0,4,3,1:T(8,128)}, f32[32,1,384,512,1]{2,0,4,3,1:T(8,128)}) fusion(f32[32,1,384,512,2]{2,0,4,3,1:T(8,128)} %bitcast.164), kind=kLoop, calls=%fused_computation.110 | loop fusion | bytes 100663296 | tf_op jit(solution)/shard_map/jvp()/slice | solution.py:13
  823.3 24.9 copy.108
  848.3 30.8 fusion.7
  892.3 65.5 %gather_fusion.1 = f32[8192]{0:T(1024)S(1)} fusion(f32[1024,32]{0,1:T(8,128)S(1)} %convolution_add_fusion, s32[8192]{0:T(1024)S(1)} %reshape.441), kind=kCustom, calls=%fused_computation.5 | custom fusion | bytes 131072 | tf_op jit(solution)/shard_map/jit(take_along_axis)/gather | solution.py:32
  958.3 62.4 %gather_fusion.4 = bf16[12288,1024]{1,0:T(8,128)(2,1)} fusion(bf16[1024,1024]{1,0:T(8,128)(2,1)} %param.15, s32[12288]{0:T(1024)S(1)} %copy-done.13), kind=kCustom, calls=%fused_computation.2.clone | custom fusion | bytes 50380800 | tf_op jit(solution)/shard_map/jit(_take)/gather | solution.py:49
  1020.8 385.8 %all-to-all-done.1 = bf16[32,384,1024]{2,1,0:T(8,128)(2,1)} async-done(((bf16[32,384,1024]{2,1,0:T(8,128)(2,1)}), bf16[32,384,1024]{2,1,0:T(8,128)(2,1)}, u32[]{:S(2)}, u32[]{:S(2)}) %all-to-all-start.1) | async-done | bytes 25165856 | tf_op jit(solution)/shard_map/all_to_all | solution.py:40
  1406.6 52.1 %gather_fusion.3 = bf16[8192,1024]{1,0:T(8,128)(2,1)} fusion(bf16[12288,1024]{1,0:T(8,128)(2,1)} %bitcast.18, s32[8192]{0:T(1024)S(1)} %broadcast_clamp_fusion.1), kind=kCustom, calls=%fused_computation.1.clone | custom fusion | bytes 33587200 | tf_op jit(solution)/shard_map/jit(_take)/gather | solution.py:41
  1474.4 68.0 %gather_fusion = f32[12288]{0:T(1024)S(1)} fusion(f32[8192]{0:T(1024)S(1)} %div.61, s32[12288]{0:T(1024)S(1)} %copy-done.22), kind=kCustom, calls=%fused_computation.4 | custom fusion | bytes 147456 | tf_op jit(solution)/shard_map/jit(_take)/gather | solution.py:48
  1556.9 583.9 %all_to_all.40 = bf16[32,384,1024]{2,1,0:T(8,128)(2,1)} all-to-all(bf16[32,384,1024]{2,1,0:T(8,128)(2,1)S(1)} %bitcast.165), channel_id=1, replica_groups=mesh['ep'=32] {'ep'}, dimensions={0} | all-to-all | bytes 50331648 | tf_op jit(solution)/shard_map/all_to_all | solution.py:51
  2140.8 49.9 %fusion.15 = (f32[32,1,384,512,1]{3,2,0,4,1:T(8,128)}, f32[32,1,384,512,1]{3,2,0,4,1:T(8,128)}) fusion(f32[32,1,384,512,1]{3,2,0,4,1:T(8,128)} %copy.109, f32[32,1,384,512,1]{3,2,0,4,1:T(8,128)} %copy.108, bf16[32,384,1024]{2,1,0:T(8,128)(2,1)} %all_to_all.40, bf16[1,512,1024]{2,1,0:T(8,128)(2,1)S(1)} %copy-done.30), kind=kOutput, calls=%fused_computation.36 | convolution fusion | flops 13092519936 | bytes 126877696 | tf_op jit(solution)/shard_map/secd,efd->secf/dot_general | solution.py:54
  2190.7 28.8 convert_reduce_fusion.1
  2219.5 32.2 %copy.97 = bf16[32,1,384,512,2]{2,0,4,3,1:T(8,128)(2,1)} copy(bf16[32,1,384,512,2]{3,2,0,4,1:T(8,128)(2,1)} %get-tuple-element.13) | data formatting | bytes 50331648 | tf_op jit(solution)/shard_map/convert_element_type | solution.py:55
  2251.7 31.6 %copy.98 = bf16[32,384,1024]{2,1,0:T(8,128)(2,1)} copy(bf16[32,384,1024]{1,0,2:T(8,128)(2,1)} %bitcast.166) | data formatting | bytes 50331648 | tf_op jit(solution)/shard_map/convert_element_type | solution.py:55
  2283.3 38.2 %convolution_convert_fusion = bf16[32,384,1024]{2,1,0:T(8,128)(2,1)} fusion(bf16[32,384,1024]{2,1,0:T(8,128)(2,1)} %copy.98, bf16[1,1024,1024]{2,1,0:T(8,128)(2,1)S(1)} %copy-done), kind=kOutput, calls=%fused_computation.50 | convolution fusion | flops 25782386688 | bytes 52428800 | tf_op jit(solution)/shard_map/secf,edf->secd/dot_general | solution.py:58
  2336.6 569.5 %psum.15 = f32[32]{0:T(128)} all-reduce(f32[32]{0:T(128)S(1)} %convert_reduce_fusion.3), channel_id=1, replica_groups=mesh['ep'=32] {'ep'}, use_global_device_ids=true, to_apply=%region_9.12 | all-reduce | flops 32 | bytes 256 | tf_op jit(solution)/shard_map/psum | solution.py:64
  2921.3 33.0 %convolution_bitcast_fusion = f32[1,1024,1024]{2,1,0:T(8,128)} fusion(bf16[32,384,1024]{2,1,0:T(8,128)(2,1)} %all_to_all.39, bf16[32,384,1024]{2,1,0:T(8,128)(2,1)} %copy.98), kind=kOutput, calls=%fused_computation.56 | convolution fusion | flops 25769803776 | bytes 54525952 | tf_op jit(solution)/shard_map/secd,secf->edf/dot_general | solution.py:57
  2954.3 35.2 %fusion.28 = f32[1,512,1024]{2,1,0:T(8,128)} fusion(bf16[32,384,1024]{2,1,0:T(8,128)(2,1)} %all_to_all.40, f32[32,1,384,512,1]{3,2,0,4,1:T(8,128)} %copy.108, f32[32,1,384,512,1]{3,2,0,4,1:T(8,128)} %copy.109), kind=kOutput, calls=%fused_computation.59 | convolution fusion | flops 12947816448 | bytes 77594624 | tf_op jit(solution)/shard_map/secf,secd->efd/dot_general | solution.py:53
  2989.6 52.2 %gather_fusion.5 = bf16[8192,1024]{1,0:T(8,128)(2,1)} fusion(bf16[12288,1024]{1,0:T(8,128)(2,1)} %bitcast.34, s32[8192]{0:T(1024)S(1)} %copy-done.2), kind=kCustom, calls=%fused_computation.3.clone | custom fusion | bytes 33587200 | tf_op jit(solution)/shard_map/jit(_take)/gather | solution.py:60
  3041.8 26.1 convert_reduce_fusion.2
  (110 shorter events, 117.5 us)
Async XLA Ops:
  7.2 673.1 %copy-start = (bf16[1,1024,1024]{2,1,0:T(8,128)(2,1)S(1)}, bf16[1,1024,1024]{2,1,0:T(8,128)(2,1)}, u32[]{:S(2)}) copy-start(bf16[1,1024,1024]{2,1,0:T(8,128)(2,1)} %param.20) | copy-start | bytes 6291460
  8.7 94.2 %copy-start.18 = (s32[1024,8]{0,1:T(8,128)}, s32[1024,8]{0,1:T(8,128)S(1)}, u32[]{:S(2)}) copy-start(s32[1024,8]{0,1:T(8,128)S(1)} %get-tuple-element.17) | copy-start | bytes 98308
  39.8 63.2 %copy-start.8 = (s32[12289]{0:T(1024)}, s32[12289]{0:T(1024)S(1)}, u32[]{:S(2)}) copy-start(s32[12289]{0:T(1024)S(1)} %scatter_custom_fusion) | copy-start | bytes 147472
  39.8 63.1 %copy-start.24 = (pred[12288]{0:T(1024)(128)(4,1)}, pred[12288]{0:T(1024)(128)(4,1)S(1)}, u32[]{:S(2)}) copy-start(pred[12288]{0:T(1024)(128)(4,1)S(1)} %compare_and_fusion) | copy-start | bytes 36868
  40.5 62.4 %copy-start.12 = (s32[12288]{0:T(1024)}, s32[12288]{0:T(1024)S(1)}, u32[]{:S(2)}) copy-start(s32[12288]{0:T(1024)S(1)} %get-tuple-element.23) | copy-start | bytes 147460
  115.2 565.1 %copy-start.31 = (f32[1,1024]{1,0:T(1,128)S(1)}, f32[1,1024]{1,0:T(1,128)}, u32[]{:S(2)}) copy-start(f32[1,1024]{1,0:T(1,128)} %param.21) | copy-start | bytes 12292
  823.3 24.9 copy-start.29
  823.3 24.9 copy-start.32
  879.1 527.5 %all-to-all-start.1 = ((bf16[32,384,1024]{2,1,0:T(8,128)(2,1)}), bf16[32,384,1024]{2,1,0:T(8,128)(2,1)}, u32[]{:S(2)}, u32[]{:S(2)}) async-start(bf16[32,384,1024]{2,1,0:T(8,128)(2,1)} %fusion.7), calls=%async_computation.1 | async-start | bytes 50331648 | tf_op jit(solution)/shard_map/all_to_all | solution.py:40
  892.2 66.0 %copy-start.13 = (s32[12288]{0:T(1024)S(1)}, s32[12288]{0:T(1024)}, u32[]{:S(2)}) copy-start(s32[12288]{0:T(1024)} %copy-done.12) | copy-start | bytes 147460
  958.3 62.4 %copy-start.6 = (s32[1024,8]{0,1:T(8,128)S(1)}, s32[1024,8]{0,1:T(8,128)}, u32[]{:S(2)}) copy-start(s32[1024,8]{0,1:T(8,128)} %param.18) | copy-start | bytes 98308
  958.3 62.4 %copy-start.23 = (s32[8192]{0:T(1024)S(1)}, s32[8192]{0:T(1024)}, u32[]{:S(2)}) copy-start(s32[8192]{0:T(1024)} %reshape.469) | copy-start | bytes 98308
  1020.7 437.9 %copy-start.1 = (s32[8192]{0:T(1024)}, s32[8192]{0:T(1024)S(1)}, u32[]{:S(2)}) copy-start(s32[8192]{0:T(1024)S(1)} %broadcast_clamp_fusion.1) | copy-start | bytes 98308
  1406.6 52.1 %copy-start.10 = (pred[1024,8]{1,0:T(8,128)(4,1)S(1)}, pred[1024,8]{1,0:T(8,128)(4,1)}, u32[]{:S(2)}) copy-start(pred[1024,8]{1,0:T(8,128)(4,1)} %copy.89) | copy-start | bytes 24580
  1474.0 68.5 %copy-start.3 = (f32[1024,8]{1,0:T(8,128)}, f32[1024,8]{1,0:T(8,128)S(1)}, u32[]{:S(2)}) copy-start(f32[1024,8]{1,0:T(8,128)S(1)} %copy.88) | copy-start | bytes 98308
  1474.4 68.1 %copy-start.9 = (s32[12289]{0:T(1024)S(1)}, s32[12289]{0:T(1024)}, u32[]{:S(2)}) copy-start(s32[12289]{0:T(1024)} %copy-done.8) | copy-start | bytes 147472
  1474.4 68.1 %copy-start.25 = (pred[12288]{0:T(1024)(128)(4,1)S(1)}, pred[12288]{0:T(1024)(128)(4,1)}, u32[]{:S(2)}) copy-start(pred[12288]{0:T(1024)(128)(4,1)} %copy-done.24) | copy-start | bytes 36868
  1556.9 583.9 %copy-start.30 = (bf16[1,512,1024]{2,1,0:T(8,128)(2,1)S(1)}, bf16[1,512,1024]{2,1,0:T(8,128)(2,1)}, u32[]{:S(2)}) copy-start(bf16[1,512,1024]{2,1,0:T(8,128)(2,1)} %param.22) | copy-start | bytes 3145732
  2321.5 668.1 %all-to-all-start.3 = ((bf16[32,384,1024]{2,1,0:T(8,128)(2,1)}), bf16[32,384,1024]{2,1,0:T(8,128)(2,1)}, u32[]{:S(2)}, u32[]{:S(2)}) async-start(bf16[32,384,1024]{2,1,0:T(8,128)(2,1)} %convolution_convert_fusion), calls=%async_computation.3 | async-start | bytes 50331648 | tf_op jit(solution)/shard_map/all_to_all | solution.py:59
  2336.3 733.7 %all-reduce.4.cloned.1.call-start = ((), (), s32[]{:S(2)}) async-start(), calls=%async_computation.4 | async-start | bytes 262144 | tf_op jit(solution)/shard_map/psum | solution.py:63
  2954.3 35.3 %copy-start.2 = (s32[8192]{0:T(1024)S(1)}, s32[8192]{0:T(1024)}, u32[]{:S(2)}) copy-start(s32[8192]{0:T(1024)} %copy-done.1) | copy-start | bytes 98308
  2989.6 52.2 %copy-start.4 = (f32[1024,8]{1,0:T(8,128)S(1)}, f32[1024,8]{1,0:T(8,128)}, u32[]{:S(2)}) copy-start(f32[1024,8]{1,0:T(8,128)} %copy-done.3) | copy-start | bytes 98308
  2989.6 52.2 %copy-start.11 = (pred[1024,8]{1,0:T(8,128)(4,1)S(1)}, pred[1024,8]{1,0:T(8,128)(4,1)}, u32[]{:S(2)}) copy-start(pred[1024,8]{1,0:T(8,128)(4,1)} %copy.89) | copy-start | bytes 24580
  3041.8 26.1 copy-start.21
  (12 other events, 126.3 us)
Sparse Core Ops, SparseCore 0:
  2909.0 128.8 all-reduce.3
where the time goes:
time: 3090 us; the launch traced here: 3080 us
  blocking collectives  1720 us (56%)
  local copies, waits for them, and re-layouts  595 us (19%)
  waiting for transfers between devices  386 us (12%)
  matrix products  245 us (8%)
  other arithmetic  96.3 us (3%)
    all_to_all x1, blocking collectives, local_block(): lax.all_to_all(send_q, 'ep', 0, 0, tiled=True)  584 us
    psum x1, blocking collectives, local_block(): lax.psum(jnp.sum(logit_grad, axis=0, dtype=jnp.float32), 'ep')  570 us
    all_to_all x1, blocking collectives, local_block(): lax.all_to_all(send_x, 'ep', 0, 0, tiled=True)  565 us
    all_to_all x1, waiting for transfers between devices, local_block(): lax.all_to_all(y_rows.reshape(buf_rows, d_model), 'ep', 0, 0, tiled=True)  386 us
    gather x1, local copies, waits for them, and re-layouts, local_block(): jnp.take(gate_w.reshape(-1), src_copy, axis=0, mode='fill', fill_value=0)  68 us
    gather x5, local copies, waits for them, and re-layouts, local_block(): jnp.take_along_axis(logits, expert_ids, axis=1)  66.4 us
    convert_element_type x2, local copies, waits for them, and re-layouts, local_block(): pre_grad = act_vjp(act_grad)[0].astype(jnp.bfloat16)  63.8 us
    gather x1, local copies, waits for them, and re-layouts, local_block(): send_x = jnp.take(hidden, src_tok, axis=0, mode='fill', fill_value=0)  62.4 us
  transfers between devices with their start and end apart: 3, of which 1 were waited for; matrix products, arithmetic and copies ran while one was open for 10% of the time, Pallas kernels for 0%

commit v1 on v0

v1 whole, which is shorter than its diff:
```python
import functools

import jax
import jax.numpy as jnp
from jax import lax
from jax.experimental import pallas as pl
from jax.experimental.pallas import tpu as pltpu
from jax.sharding import PartitionSpec as P

LIMIT = 7.0
ALPHA = 1.702
F32 = jnp.float32
BF16 = jnp.bfloat16
PLANE = 8
DEPTH = 4
VMEM_LIMIT = 62 * 1024 * 1024


def dot(a, b, dims=((1,), (0,))):
    return lax.dot_general(a, b, (dims, ((), ())), preferred_element_type=F32)


def place(me):
    c = me % PLANE
    core, xb, yb = c % 2, (c // 2) % 2, c // 4
    return c, me + 1 - 2 * core, me + 2 - 4 * xb, me + 4 - 8 * yb


def gather_kernel(world, x_ref, dy_ref, meta_ref, bias_ref, xall, dyall, metaall, biasall,
                  send, recv, msend, mrecv, bsend, brecv, local):
    me = lax.axis_index('ep')
    c, partner, xn, yn = place(me)
    base = me - c
    plane_peers = [base + (c + k) % PLANE for k in range(1, PLANE)]
    col_peers = [(me + PLANE * k) % world for k in range(1, DEPTH)]
    cx, cy = xn - base, yn - base
    cd = cx + cy - c
    half = x_ref.shape[0] // 2

    barrier = pltpu.get_barrier_semaphore()
    for peer in plane_peers + col_peers:
        pl.semaphore_signal(barrier, inc=1, device_id=(peer,), device_id_type=pl.DeviceIdType.MESH)
    pl.semaphore_wait(barrier, len(plane_peers) + len(col_peers))

    refs = ((x_ref, xall), (dy_ref, dyall))

    def copy(a, kind, src, blk, h, dev):
        rows = pl.ds(h * half, half)
        source = refs[a][0].at[rows] if src is None else refs[a][1].at[src, rows]
        return pltpu.make_async_remote_copy(
            src_ref=source, dst_ref=refs[a][1].at[blk, rows],
            send_sem=send.at[a, kind], recv_sem=recv.at[a, kind],
            device_id=(dev,), device_id_type=pl.DeviceIdType.MESH)

    started = []

    def go(cp):
        cp.start()
        started.append(cp)

    mine = [pltpu.make_async_copy(refs[a][0], refs[a][1].at[c], local.at[a]) for a in range(2)]
    mine.append(pltpu.make_async_copy(meta_ref.at[c], metaall.at[c], local.at[2]))
    mine.append(pltpu.make_async_copy(bias_ref, biasall.at[me // PLANE], local.at[3]))
    for a in range(2):
        go(copy(a, 0, None, c, 0, xn))
        go(copy(a, 3, None, c, 1, yn))
        go(copy(a, 1, None, c, 1, xn))
        go(copy(a, 2, None, c, 0, yn))
    for k, peer in enumerate(plane_peers):
        go(pltpu.make_async_remote_copy(
            src_ref=meta_ref.at[peer - base], dst_ref=metaall.at[c], send_sem=msend.at[k],
            recv_sem=mrecv.at[k], device_id=(peer,), device_id_type=pl.DeviceIdType.MESH))
    for k, peer in enumerate(col_peers):
        go(pltpu.make_async_remote_copy(
            src_ref=bias_ref, dst_ref=biasall.at[me // PLANE], send_sem=bsend.at[k],
            recv_sem=brecv.at[k], device_id=(peer,), device_id_type=pl.DeviceIdType.MESH))
    for m in mine:
        m.start()
    for a in range(2):
        go(copy(a, 6, None, c, 0, partner))
        go(copy(a, 7, None, c, 1, partner))

    def arrived(a, kind, blk, h):
        copy(a, kind, blk, blk, h, partner).wait_recv()

    for a in range(2):
        arrived(a, 0, cx, 0)
        go(copy(a, 4, cx, cx, 0, yn))
        go(copy(a, 8, cx, cx, 0, partner))
        arrived(a, 3, cy, 1)
        go(copy(a, 5, cy, cy, 1, xn))
        go(copy(a, 11, cy, cy, 1, partner))
        arrived(a, 1, cx, 1)
        go(copy(a, 9, cx, cx, 1, partner))
        arrived(a, 2, cy, 0)
        go(copy(a, 10, cy, cy, 0, partner))
    for a in range(2):
        arrived(a, 4, cd, 0)
        go(copy(a, 12, cd, cd, 0, partner))
        arrived(a, 5, cd, 1)
        go(copy(a, 13, cd, cd, 1, partner))
    flip = partner - me
    for a in range(2):
        for n, blk in enumerate((c, cx, cy, cd)):
            for h in range(2):
                arrived(a, 6 + 2 * n + h, blk + flip, h)
    for k, peer in enumerate(plane_peers):
        pltpu.make_async_remote_copy(
            src_ref=meta_ref.at[c], dst_ref=metaall.at[(c + PLANE - k - 1) % PLANE], send_sem=msend.at[k],
            recv_sem=mrecv.at[k], device_id=(peer,), device_id_type=pl.DeviceIdType.MESH).wait_recv()
    for k, peer in enumerate(col_peers):
        pltpu.make_async_remote_copy(
            src_ref=bias_ref, dst_ref=biasall.at[(me // PLANE + DEPTH - k - 1) % DEPTH], send_sem=bsend.at[k],
            recv_sem=brecv.at[k], device_id=(peer,), device_id_type=pl.DeviceIdType.MESH).wait_recv()
    for cp in started:
        cp.wait_send()
    for m in mine:
        m.wait()


def gather_call(world, x, dy, meta, bias):
    tok, d = x.shape
    any_spec = pl.BlockSpec(memory_space=pl.ANY)
    vmem = pl.BlockSpec(memory_space=pltpu.VMEM)
    blocks = jax.ShapeDtypeStruct((PLANE, tok, d), x.dtype)
    dma = pltpu.SemaphoreType.DMA
    return pl.pallas_call(
        functools.partial(gather_kernel, world),
        in_specs=[vmem] * 4,
        out_specs=[any_spec] * 4,
        out_shape=[blocks, blocks, jax.ShapeDtypeStruct(meta.shape, F32),
                   jax.ShapeDtypeStruct((DEPTH,) + bias.shape, F32)],
        scratch_shapes=[dma((2, 14)), dma((2, 14)), dma((PLANE - 1,)), dma((PLANE - 1,)),
                        dma((DEPTH - 1,)), dma((DEPTH - 1,)), dma((4,))],
        compiler_params=pltpu.CompilerParams(collective_id=0, has_side_effects=True, vmem_limit_bytes=24 * 2**20),
        cost_estimate=pl.CostEstimate(flops=100 * 10**9, bytes_accessed=40 * 2**20, transcendentals=0),
        name="plane_gather",
    )(x, dy, meta, bias)


def rows_kernel(cap, meta_ref, x_ref, dy_ref, xr_ref, qr_ref):
    tok = x_ref.shape[1]
    slot_iota = lax.broadcasted_iota(jnp.int32, (cap, tok), 0).astype(F32)
    for e in range(DEPTH):
        hit = meta_ref[0, e:e + 1, :] == slot_iota
        sel = jnp.where(hit, 1.0, 0.0).astype(BF16)
        w_row = jnp.sum(jnp.where(hit, meta_ref[0, DEPTH + e:DEPTH + e + 1, :], 0.0), axis=1, keepdims=True)
        xr_ref[e] = dot(sel, x_ref[0]).astype(BF16)
        qr_ref[e] = (w_row * dot(sel, dy_ref[0])).astype(BF16)


def rows_call(meta, x_all, dy_all, cap):
    srcs, tok, d = x_all.shape
    tok_spec = pl.BlockSpec((1, tok, d), lambda s: (s, 0, 0))
    row_spec = pl.BlockSpec((DEPTH, cap, d), lambda s: (0, s, 0))
    row_shape = jax.ShapeDtypeStruct((DEPTH, srcs * cap, d), BF16)
    return pl.pallas_call(
        functools.partial(rows_kernel, cap),
        grid=(srcs,),
        in_specs=[pl.BlockSpec((1, 2 * DEPTH, tok), lambda s: (s, 0, 0)), tok_spec, tok_spec],
        out_specs=[row_spec, row_spec],
        out_shape=[row_shape, row_shape],
        compiler_params=pltpu.CompilerParams(dimension_semantics=("arbitrary",), vmem_limit_bytes=VMEM_LIMIT),
        cost_estimate=pl.CostEstimate(flops=4 * srcs * DEPTH * cap * d * tok, bytes_accessed=90 * 2**20, transcendentals=0),
        name="rows",
    )(meta, x_all, dy_all)


def swiglu_parts(h, ff):
    gate_in = h[:, :ff]
    up_in = h[:, ff:]
    g = jnp.minimum(gate_in, LIMIT)
    u1 = jnp.clip(up_in, -LIMIT, LIMIT) + 1.0
    sg = 1.0 / (1.0 + jnp.exp(-ALPHA * g))
    return gate_in, up_in, u1, sg, g * sg


def down_kernel(ff, xr_ref, qr_ref, wgu_ref, bgu_ref, act_ref, dwd_ref):
    h = dot(xr_ref[0], wgu_ref[0]) + bgu_ref[0]
    _, _, u1, _, gs = swiglu_parts(h, ff)
    act = (gs * u1).astype(BF16)
    act_ref[0] = act
    q = qr_ref[0]
    dwd = dot(act, q, ((0,), (0,)))
    dbd = jnp.broadcast_to(jnp.sum(q.astype(F32), axis=0, keepdims=True), (8, q.shape[1]))
    step = pl.program_id(1)

    @pl.when(step == 0)
    def _():
        dwd_ref[0, :ff] = dwd
        dwd_ref[0, ff:] = dbd

    @pl.when(step > 0)
    def _():
        dwd_ref[0, :ff] += dwd
        dwd_ref[0, ff:] += dbd


def down_call(x_rows, q_rows, wgu, bgu, tile):
    experts, rows, d = x_rows.shape
    ff2 = wgu.shape[2]
    ff = ff2 // 2
    per_e = lambda a, b: pl.BlockSpec((1, a, b), lambda e, s: (e, 0, 0))
    row_spec = pl.BlockSpec((1, tile, d), lambda e, s: (e, s, 0))
    return pl.pallas_call(
        functools.partial(down_kernel, ff),
        grid=(experts, rows // tile),
        in_specs=[row_spec, row_spec, per_e(d, ff2), per_e(1, ff2)],
        out_specs=[pl.BlockSpec((1, tile, ff), lambda e, s: (e, s, 0)), per_e(ff + 8, d)],
        out_shape=[jax.ShapeDtypeStruct((experts, rows, ff), BF16),
                   jax.ShapeDtypeStruct((experts, ff + 8, d), F32)],
        compiler_params=pltpu.CompilerParams(dimension_semantics=("arbitrary", "arbitrary"), vmem_limit_bytes=VMEM_LIMIT),
        cost_estimate=pl.CostEstimate(flops=3 * experts * rows * d * ff2, bytes_accessed=80 * 2**20, transcendentals=0),
        name="down_grad",
    )(x_rows, q_rows, wgu, bgu)


def up_kernel(ff, cap, meta_ref, dy_ref, xr_ref, qr_ref, act_ref, wgu_ref, wd_ref, bgu_ref, bd_ref,
              y_ref, p_ref, dwgu_ref, r_ref, dhs):
    tile = xr_ref.shape[1]
    half = tile // 2
    for i in range(2):
        rows = pl.ds(i * half, half)
        h = dot(xr_ref[0, rows, :], wgu_ref[0]) + bgu_ref[0]
        gate_in, up_in, u1, sg, gs = swiglu_parts(h, ff)
        da = dot(qr_ref[0, rows, :], wd_ref[0], ((1,), (1,)))
        pass_g = jnp.where(gate_in < LIMIT, 1.0, jnp.where(gate_in == LIMIT, 0.5, 0.0))
        up_abs = jnp.abs(up_in)
        pass_u = jnp.where(up_abs < LIMIT, 1.0, jnp.where(up_abs == LIMIT, 0.5, 0.0))
        dhs[rows, :ff] = ((da * u1) * (sg + ALPHA * gs * (1.0 - sg)) * pass_g).astype(BF16)
        dhs[rows, ff:] = (da * gs * pass_u).astype(BF16)
        p_ref[0, rows, :] = dot(dhs[rows, :], wgu_ref[0], ((1,), (1,))).astype(BF16)
        y_ref[0, rows, :] = (dot(act_ref[0, rows, :], wd_ref[0]) + bd_ref[0]).astype(BF16)
    dh = dhs[...]
    dwgu = dot(xr_ref[0], dh, ((0,), (0,)))
    d = dwgu.shape[0]
    dbgu = jnp.broadcast_to(jnp.sum(dh.astype(F32), axis=0, keepdims=True), (8, 2 * ff))
    step = pl.program_id(1)

    @pl.when(step == 0)
    def _():
        dwgu_ref[0, :d] = dwgu
        dwgu_ref[0, d:] = dbgu

    @pl.when(step > 0)
    def _():
        dwgu_ref[0, :d] += dwgu
        dwgu_ref[0, d:] += dbgu


def up_call(x_rows, q_rows, act, wgu, wd, bgu, bd, tile):
    experts, rows, d = x_rows.shape
    ff2 = wgu.shape[2]
    ff = ff2 // 2
    per_e = lambda a, b: pl.BlockSpec((1, a, b), lambda e, s: (e, 0, 0))
    row_spec = pl.BlockSpec((1, tile, d), lambda e, s: (e, s, 0))
    row_shape = jax.ShapeDtypeStruct((experts, rows, d), BF16)

    def body(xr, qr, a, w1, w2, b1, b2, y, p, dw, dhs):
        up_kernel(ff, 0, None, None, xr, qr, a, w1, w2, b1, b2, y, p, dw, None, dhs)

    return pl.pallas_call(
        body,
        grid=(experts, rows // tile),
        in_specs=[row_spec, row_spec, pl.BlockSpec((1, tile, ff), lambda e, s: (e, s, 0)),
                  per_e(d, ff2), per_e(ff, d), per_e(1, ff2), per_e(1, d)],
        out_specs=[row_spec, row_spec, per_e(d + 8, ff2)],
        out_shape=[row_shape, row_shape, jax.ShapeDtypeStruct((experts, d + 8, ff2), F32)],
        scratch_shapes=[pltpu.VMEM((tile, ff2), BF16)],
        compiler_params=pltpu.CompilerParams(dimension_semantics=("arbitrary", "arbitrary"), vmem_limit_bytes=VMEM_LIMIT),
        cost_estimate=pl.CostEstimate(flops=8 * experts * rows * d * ff2, bytes_accessed=140 * 2**20, transcendentals=0),
        name="up_grad",
    )(x_rows, q_rows, act, wgu, wd, bgu, bd)


def combine_kernel(cap, chunk, meta_ref, dy_hbm, y_hbm, p_hbm, out_ref, dx_ref, r_ref, core_in, link_in,
                   stage, ybuf, pbuf, dybuf, ysem, psem, dysem, csend, crecv, lsend, lrecv, loads):
    me = lax.axis_index('ep')
    c, partner, xn, yn = place(me)
    base = me - c
    core, xb, yb = c % 2, (c // 2) % 2, c // 4
    half = out_ref.shape[0] // 2
    d = out_ref.shape[1]

    barrier = pltpu.get_barrier_semaphore()
    for peer in (partner, xn, yn):
        pl.semaphore_signal(barrier, inc=1, device_id=(peer,), device_id_type=pl.DeviceIdType.MESH)
    pl.semaphore_wait(barrier, 3)

    def where(t):
        u, mine = t // 2, t % 2
        v, i = u // 2, u % 2
        diag = 1 - (v + 3) // 4
        side = ((v + 1) // 2) % 2
        isx, isy = diag + side * (1 - i), diag + side * i
        swap = (v // 2) * (1 - v // 3)
        h = i + swap * (1 - 2 * i)
        dest = c + isx * (2 - 4 * xb) + isy * (4 - 8 * yb) + (1 - mine) * (1 - 2 * core)
        slot = mine * (u % 6) + (1 - mine) * (6 + u % 2)
        return dest, h, mine, slot

    def fetch(t):
        dest, h, _, _ = where(t)
        b = t % 2
        return (pltpu.make_async_copy(y_hbm.at[:, pl.ds(dest * cap, cap), :], ybuf.at[b], ysem.at[b]),
                pltpu.make_async_copy(p_hbm.at[:, pl.ds(dest * cap, cap), :], pbuf.at[b], psem.at[b]),
                pltpu.make_async_copy(dy_hbm.at[dest, pl.ds(h * half, half), :], dybuf.at[b], dysem.at[b]))

    def to_core(u):
        return pltpu.make_async_remote_copy(
            src_ref=stage.at[6 + u % 2], dst_ref=core_in.at[u], send_sem=csend.at[u], recv_sem=crecv.at[u],
            device_id=(partner,), device_id_type=pl.DeviceIdType.MESH)

    def to_link(u):
        return pltpu.make_async_remote_copy(
            src_ref=stage.at[u], dst_ref=link_in.at[u], send_sem=lsend.at[u], recv_sem=lrecv.at[u],
            device_id=((xn, yn, xn, yn, xn, yn)[u],), device_id_type=pl.DeviceIdType.MESH)

    def load(src, slot, s):
        cp = pltpu.make_async_copy(src, stage.at[slot], loads.at[s])
        cp.start()
        return cp

    def add_into(slot, other):
        @pl.loop(0, half // chunk)
        def _(k):
            rows = pl.ds(pl.multiple_of(k * chunk, chunk), chunk)
            stage[slot, 0, rows, :] += stage[other, 0, rows, :]
            stage[slot, 1, rows, :] += stage[other, 1, rows, :]

    def before(t):
        u, mine = t // 2, t % 2
        if mine:
            to_core(u).wait_recv()
            load(core_in.at[u], u % 6, 0).wait()
            if u in (4, 5):
                other = 5 - u
                to_link(other).wait_recv()
                to_link(other).wait_send()
                load(link_in.at[other], other, 1).wait()
                add_into(u, other)
        elif u >= 2:
            to_core(u - 2).wait_send()

    def after(t):
        u, mine = t // 2, t % 2
        if not mine:
            to_core(u).start()
        elif u < 6:
            to_link(u).start()

    for cp in fetch(0):
        cp.start()
    slot_iota = lax.broadcasted_iota(jnp.int32, (chunk, cap), 1).astype(F32)
    lane = lax.broadcasted_iota(jnp.int32, (chunk, 8), 1)

    @pl.loop(0, 16)
    def _(t):
        dest, h, mine, slot = where(t)
        b = t % 2
        for cp in fetch(t):
            cp.wait()

        @pl.when(t < 15)
        def _():
            for cp in fetch(t + 1):
                cp.start()

        for k in range(16):
            @pl.when(t == k)
            def _():
                before(k)

        @pl.loop(0, half // chunk)
        def _(k):
            rows = pl.ds(pl.multiple_of(k * chunk, chunk), chunk)
            tokens = pl.ds(pl.multiple_of(h * half + k * chunk, chunk), chunk)
            meta = meta_ref[dest, tokens, :]
            dy = dybuf[b, rows, :].astype(F32)
            out = jnp.zeros((chunk, d), F32)
            dx = jnp.zeros((chunk, d), F32)
            r = jnp.zeros((chunk, 8), F32)
            for j in range(DEPTH):
                sel = jnp.where(meta[:, j:j + 1] == slot_iota, 1.0, 0.0).astype(BF16)
                y = dot(sel, ybuf[b, j])
                out += meta[:, DEPTH + j:DEPTH + j + 1] * y
                r = jnp.where(lane == j, jnp.sum(dy * y, axis=1, keepdims=True), r)
                dx += dot(sel, pbuf[b, j])
            r_ref[dest, tokens, :] = r

            @pl.when(mine == 0)
            def _():
                stage[slot, 0, rows, :] = out
                stage[slot, 1, rows, :] = dx

            @pl.when(mine == 1)
            def _():
                stage[slot, 0, rows, :] += out
                stage[slot, 1, rows, :] += dx

        for k in range(16):
            @pl.when(t == k)
            def _():
                after(k)

    for slot, (first, second) in ((0, (2, 5)), (1, (4, 3))):
        for n in (first, second):
            to_link(n).wait_recv()
            to_link(n).wait_send()
            load(link_in.at[n], n, 1).wait()
            add_into(slot, n)
        out_ref[pl.ds(slot * half, half), :] = stage[slot, 0].astype(BF16)
        dx_ref[pl.ds(slot * half, half), :] = stage[slot, 1]
    to_core(6).wait_send()
    to_core(7).wait_send()


def combine_call(meta_t, dy_all, y_rows, p_rows, cap):
    srcs, tok, d = dy_all.shape
    half = tok // 2
    any_spec = pl.BlockSpec(memory_space=pl.ANY)
    vmem = pl.BlockSpec(memory_space=pltpu.VMEM)
    dma = pltpu.SemaphoreType.DMA
    chunk = min(128, half)
    return pl.pallas_call(
        functools.partial(combine_kernel, cap, chunk),
        in_specs=[vmem, any_spec, any_spec, any_spec],
        out_specs=[vmem, vmem, vmem, any_spec, any_spec],
        out_shape=[jax.ShapeDtypeStruct((tok, d), BF16), jax.ShapeDtypeStruct((tok, d), F32),
                   jax.ShapeDtypeStruct((srcs, tok, 8), F32),
                   jax.ShapeDtypeStruct((8, 2, half, d), F32), jax.ShapeDtypeStruct((6, 2, half, d), F32)],
        scratch_shapes=[pltpu.VMEM((8, 2, half, d), F32),
                        pltpu.VMEM((2, DEPTH, cap, d), BF16), pltpu.VMEM((2, DEPTH, cap, d), BF16),
                        pltpu.VMEM((2, half, d), BF16),
                        dma((2,)), dma((2,)), dma((2,)), dma((8,)), dma((8,)), dma((6,)), dma((6,)), dma((2,))],
        compiler_params=pltpu.CompilerParams(collective_id=1, has_side_effects=True, vmem_limit_bytes=67043328),
        cost_estimate=pl.CostEstimate(flops=300 * 10**9, bytes_accessed=300 * 2**20, transcendentals=0),
        name="combine_scatter",
    )(meta_t, dy_all, y_rows, p_rows)


def solution(mesh):
    world = mesh.shape['ep']
    plane_groups = [[PLANE * z + c for c in range(PLANE)] for z in range(DEPTH)]
    col_groups = [[PLANE * z + c for z in range(DEPTH)] for c in range(PLANE)]

    def local_block(hidden, grad_out, w_router, b_router, expert_ids, slot_ids, w_gate_up, b_gate_up, w_down, b_down):
        tok, d = hidden.shape
        top_k = expert_ids.shape[1]
        experts = w_router.shape[1]
        ff = w_down.shape[1]
        cap = (3 * tok * top_k + 2 * experts - 1) // (2 * experts)

        ids = jnp.arange(experts, dtype=jnp.int32)
        match = expert_ids[:, :, None] == ids
        chosen = jnp.any(match, axis=1)
        slot = jnp.max(jnp.where(match, slot_ids[:, :, None], -1), axis=1)
        logits = jnp.dot(hidden, w_router, preferred_element_type=F32) + b_router
        peak = jnp.max(jnp.where(chosen, logits, -jnp.inf), axis=1, keepdims=True)
        expd = jnp.where(chosen, jnp.exp(jnp.where(chosen, logits, peak) - peak), 0.0)
        gate = expd / jnp.sum(expd, axis=1, keepdims=True)
        meta = jnp.concatenate([slot.astype(F32).reshape(tok, DEPTH, PLANE), gate.reshape(tok, DEPTH, PLANE)], axis=1)

        col = jnp.arange(2 * ff, dtype=jnp.int32)
        perm = (col[:, None] == jnp.where(col < ff, 2 * col, 2 * (col - ff) + 1)[None, :]).astype(BF16)
        wgu = jnp.dot(w_gate_up[0], perm, preferred_element_type=F32).astype(BF16)
        bgu = b_gate_up.reshape(ff, 2).T.reshape(1, 2 * ff)
        w_cat = lax.all_gather(jnp.concatenate([wgu, w_down[0]], axis=0), 'ep', axis_index_groups=col_groups)
        bias = jnp.concatenate([bgu, b_down, jnp.zeros((6, d), F32)], axis=0)
        x_all, dy_all, meta_r, b_cat = gather_call(world, hidden, grad_out, meta.transpose(2, 1, 0), bias)
        meta_t = meta_r.transpose(0, 2, 1)
        wgu_all, wd_all, bgu_all, bd_all = w_cat[:, :d], w_cat[:, d:], b_cat[:, :1], b_cat[:, 1:2]

        x_rows, q_rows = rows_call(meta_r, x_all, dy_all, cap)
        act, dwd = down_call(x_rows, q_rows, wgu_all, bgu_all, 2 * cap)
        y_rows, p_rows, dwgu = up_call(x_rows, q_rows, act, wgu_all, wd_all, bgu_all, bd_all, 2 * cap)
        block_out, dx, r_part, _, _ = combine_call(meta_t, dy_all, y_rows, p_rows, cap)

        scatter = functools.partial(lax.psum_scatter, axis_name='ep', scatter_dimension=0, tiled=True)
        grad_wd = scatter(dwd, axis_index_groups=col_groups)
        grad_wgu = scatter(dwgu, axis_index_groups=col_groups)

        r = lax.all_to_all(r_part[:, :, :DEPTH], 'ep', 0, 0, tiled=True, axis_index_groups=plane_groups)
        r = r.transpose(1, 2, 0).reshape(tok, experts)
        sel_grad = gate * (r - jnp.sum(gate * r, axis=1, keepdims=True))
        logit_grad = sel_grad.astype(BF16)
        router_dx = lax.dot_general(logit_grad, w_router, (((1,), (1,)), ((), ())), preferred_element_type=F32)
        grad_hidden = (dx + router_dx).astype(BF16)
        grad_w_router = lax.psum(lax.dot_general(hidden, logit_grad, (((0,), (0,)), ((), ())), preferred_element_type=F32), 'ep')
        grad_b_router = lax.psum(jnp.sum(logit_grad.astype(F32), axis=0), 'ep')

        grad_w_gate_up = jnp.stack([grad_wgu[0, :d, :ff], grad_wgu[0, :d, ff:]], axis=-1).reshape(1, d, 2 * ff)
        grad_b_gate_up = grad_wgu[0, d].reshape(2, ff).T.reshape(1, 2 * ff)
        return (block_out, grad_hidden, grad_w_router, grad_b_router, grad_w_gate_up,
                grad_b_gate_up, grad_wd[:, :ff], grad_wd[:, ff])

    tok_spec = P('ep', None)
    in_specs = (tok_spec, tok_spec, P(None, None), P(None), tok_spec, tok_spec, P('ep', None, None), P('ep', None), P('ep', None, None), P('ep', None))
    out_specs = (tok_spec, tok_spec, P(None, None), P(None), P('ep', None, None), P('ep', None), P('ep', None, None), P('ep', None))
    return jax.shard_map(local_block, mesh=mesh, in_specs=in_specs, out_specs=out_specs, check_vma=False)
```

time: 3090 us -> 965 us (0.31)
  blocking collectives: 1720 us -> 38.4 us
  Pallas kernels: 0 us -> 729 us
  local copies, waits for them, and re-layouts: 595 us -> 59.9 us
  waiting for transfers between devices: 386 us -> 102 us
  matrix products: 245 us -> 10.2 us
  other arithmetic: 96.3 us -> 5.91 us
    all_to_all x2 -> x0, blocking collectives: 1150 us -> none  [the longest x1 584 us: local_block(): lax.all_to_all(send_q, 'ep', 0, 0, tiled=True)]
    pallas_call x0 -> x5, Pallas kernels: none -> 729 us  [the longest x1 332 us: combine_call(): pl.pallas_call(functools.partial(combine_kernel, cap, chunk), in_specs=[v...]
    psum x1, blocking collectives: 570 us -> 38.4 us  [local_block(): grad_b_router = lax.psum(jnp.sum(logit_grad.astype(F32), axis=0), 'ep')]
    all_to_all x2 -> x1, waiting for transfers between devices: 386 us -> 5.18 us  [local_block(): lax.all_to_all(r_part[:, :, :DEPTH], 'ep', 0, 0, tiled=True, axis_index_g...]
    gather x10 -> x0, local copies, waits for them, and re-layouts: 364 us -> none  [the longest x1 68 us: local_block(): jnp.take(gate_w.reshape(-1), src_copy, axis=0, mode='fill', fill_value=0)]
    dot_general x10 -> x4, matrix products: 245 us -> 10.2 us  [the longest x1 4.23 us: local_block(): lax.dot_general(logit_grad, w_router, (((1,), (1,)), ((), ())), preferred...]
    psum x1, waiting for transfers between devices: 0.01 us -> 97 us  [local_block(): lax.psum(lax.dot_general(hidden, logit_grad, (((0,), (0,)), ((), ())), pr...]
    reduce_sum x7 -> x3, other arithmetic: 67.2 us -> 0.37 us  [the longest x1 0.21 us: local_block(): grad_b_router = lax.psum(jnp.sum(logit_grad.astype(F32), axis=0), 'ep')]
  transfers between devices with their start and end apart: 3 -> 5, of which waited for: 1 -> 2; matrix products, arithmetic and copies ran while one was open for 10% -> 5% of each run, Pallas kernels for 0% -> 70%
where the time goes in v1:
time: 965 us; the launch traced here: 964 us
  Pallas kernels  729 us (76%)
  waiting for transfers between devices  102 us (11%)
  local copies, waits for them, and re-layouts  59.9 us (6%)
  blocking collectives  38.4 us (4%)
  between operations  14.1 us (1%)
  matrix products  10.2 us (1%)
    pallas_call x1, Pallas kernels, combine_call(): pl.pallas_call(functools.partial(combine_kernel, cap, chunk), in_specs=[v...  332 us
    pallas_call x1, Pallas kernels, gather_call(): pl.pallas_call(functools.partial(gather_kernel, world), in_specs=[vmem] *...  149 us
    pallas_call x1, Pallas kernels, up_call(): pl.pallas_call(body, grid=(experts, rows // tile), in_specs=[row_spec, ro...  134 us
    psum x1, waiting for transfers between devices, local_block(): lax.psum(lax.dot_general(hidden, logit_grad, (((0,), (0,)), ((), ())), pr...  97 us
    pallas_call x1, Pallas kernels, rows_call(): pl.pallas_call(functools.partial(rows_kernel, cap), grid=(srcs,), in_spec...  60.2 us
    pallas_call x1, Pallas kernels, down_call(): pl.pallas_call(functools.partial(down_kernel, ff), grid=(experts, rows //...  53.8 us
    psum x1, blocking collectives, local_block(): grad_b_router = lax.psum(jnp.sum(logit_grad.astype(F32), axis=0), 'ep')  38.4 us
  transfers between devices with their start and end apart: 5, of which 2 were waited for; matrix products, arithmetic and copies ran while one was open for 5% of the time, Pallas kernels for 70%

profile of v1, /device:TPU:0, one launch (start us, length us, event | category | flops | bytes accessed | tf_op | source)
XLA Modules:
  0.0 963.7 jit_solution(10496527865781381807)
XLA Ops:
  7.2 4.1 convert_bitcast_fusion
  11.4 2.0 pad_maximum_fusion.1
  17.4 1.6 copy-done.4
  19.0 149.2 %plane_gather.1 = (bf16[8,1024,1024]{2,1,0:T(8,128)(2,1)S(1)}, bf16[8,1024,1024]{2,1,0:T(8,128)(2,1)}, f32[8,8,1024]{2,1,0:T(8,128)S(1)}, f32[4,8,1024]{2,1,0:T(8,128)S(1)}) custom-call(bf16[1024,1024]{1,0:T(8,128)(2,1)S(1)} %copy-done, bf16[1024,1024]{1,0:T(8,128)(2,1)S(1)} %copy-done.4, f32[8,8,1024]{2,1,0:T(8,128)S(1)} %maximum_bitcast_fusion.meta_ref, ...), custom_call_target="tpu_custom_call" | custom-call | flops 99999997952 | bytes 41943040 | tf_op jit(solution)/shard_map/plane_gather/pallas_call | solution.py:127
  168.9 5.8 copy-done.5
  175.3 60.2 %rows.1 = (bf16[4,3072,1024]{2,1,0:T(8,128)(2,1)}, bf16[4,3072,1024]{2,1,0:T(8,128)(2,1)}) custom-call(f32[8,8,1024]{2,1,0:T(8,128)} %copy-done.2, bf16[8,1024,1024]{2,1,0:T(8,128)(2,1)} %copy-done.5, bf16[8,1024,1024]{2,1,0:T(8,128)(2,1)} %get-tuple-element.23.dy_ref.dy_hbm), custom_call_target="tpu_custom_call" | custom-call | flops 51539607552 | bytes 94371840 | tf_op jit(solution)/shard_map/rows/pallas_call | solution.py:157
  235.5 7.7 slice.40.wgu_ref.w1
  243.2 53.8 %down_grad.1 = (bf16[4,3072,512]{2,1,0:T(8,128)(2,1)}, f32[4,520,1024]{2,1,0:T(8,128)}) custom-call(bf16[4,3072,1024]{2,1,0:T(8,128)(2,1)} %get-tuple-element.25.xr_ref.xr, bf16[4,3072,1024]{2,1,0:T(8,128)(2,1)} %get-tuple-element.26.qr_ref.qr, bf16[4,1024,1024]{2,1,0:T(8,128)(2,1)} %slice.40.wgu_ref.w1, f32[4,1,1024]{2,1,0:T(1,128)} %get-tuple-element.65.bgu_ref.b1), custom_call_target="tpu_custom_call" | custom-call | flops 38654705664 | bytes 83886080 | tf_op jit(solution)/shard_map/down_grad/pallas_call | solution.py:205
  297.3 4.6 slice.41.w2
  301.9 134.1 %up_grad.1 = (bf16[4,3072,1024]{2,1,0:T(8,128)(2,1)}, bf16[4,3072,1024]{2,1,0:T(8,128)(2,1)}, f32[4,1032,1024]{2,1,0:T(8,128)}) custom-call(bf16[4,3072,1024]{2,1,0:T(8,128)(2,1)} %get-tuple-element.25.xr_ref.xr, bf16[4,3072,1024]{2,1,0:T(8,128)(2,1)} %get-tuple-element.26.qr_ref.qr, bf16[4,3072,512]{2,1,0:T(8,128)(2,1)} %get-tuple-element.28.a, ...), custom_call_target="tpu_custom_call" | custom-call | flops 103079215104 | bytes 146800640 | tf_op jit(solution)/shard_map/up_grad/pallas_call | solution.py:262
  436.9 2.7 copy.47
  439.6 331.9 %combine_scatter.1 = (bf16[1024,1024]{1,0:T(8,128)(2,1)}, f32[1024,1024]{1,0:T(8,128)}, f32[8,1024,8]{2,1,0:T(8,128)}, f32[8,2,512,1024]{3,2,1,0:T(8,128)}, f32[6,2,512,1024]{3,2,1,0:T(8,128)}) custom-call(f32[8,1024,8]{2,1,0:T(8,128)} %bitcast.52, bf16[8,1024,1024]{2,1,0:T(8,128)(2,1)} %get-tuple-element.23.dy_ref.dy_hbm, ...), custom_call_target="tpu_custom_call" | custom-call | flops 299999985664 | bytes 314572800 | tf_op jit(solution)/shard_map/combine_scatter/pallas_call | solution.py:425
  771.5 3.6 copy.48
  775.1 3.4 all-to-all-start
  778.6 5.2 all-to-all-done
  784.1 38.4 %psum.15 = f32[32]{0:T(128)} all-reduce(f32[32]{0:T(128)S(1)} %get-tuple-element.60), channel_id=1, replica_groups=mesh['ep'=32] {'ep'}, use_global_device_ids=true, to_apply=%region_7.8 | all-reduce | flops 32 | bytes 256 | tf_op jit(solution)/shard_map/psum | solution.py:490
  823.6 4.2 add_convert_fusion
  827.9 3.2 slice.45
  832.4 2.7 slice_bitcast_fusion.1
  835.1 2.5 pad_maximum_fusion
  837.5 7.3 copy.50
  844.9 6.1 reshape.58
  851.0 5.5 copy.52
  858.2 97.0 %all-reduce.2.cloned.1.call-done = f32[1024,32]{0,1:T(8,128)} async-done(((f32[1024,32]{0,1:T(8,128)}), f32[1024,32]{0,1:T(8,128)}) %all-reduce.2.cloned.1.call-update) | async-done | bytes 131088 | tf_op jit(solution)/shard_map/psum | solution.py:489
  (86 shorter events, 13.1 us)
Async XLA Ops:
  7.2 228.3 %all-gather.3.cloned.1.call-start = ((), (), s32[]{:S(2)}) async-start(), calls=%async_computation.6 | async-start | bytes 15728640 | tf_op jit(solution)/shard_map/all_gather | solution.py:468
  7.2 4.1 copy-start.11
  11.3 2.3 copy-start.15
  11.4 2.4 copy-start
  11.4 2.4 copy-start.12
  11.4 2.4 copy-start.23
  13.4 2.0 copy-start.20
  13.4 2.8 copy-start.21
  13.4 3.9 copy-start.22
  13.4 814.5 %reduce-scatter.5.cloned.1.call-start = ((), (), s32[]{:S(2)}) async-start(), calls=%async_computation.5 | async-start | bytes 10649600 | tf_op jit(solution)/shard_map/reduce_scatter | solution.py:480
  13.8 1.5 copy-start.9
  17.4 1.6 copy-start.4
  168.9 5.8 copy-start.5
  297.0 535.4 %reduce-scatter.3.cloned.1.call-start = ((), (), s32[]{:S(2)}) async-start(), calls=%async_computation.4 | async-start | bytes 21135360 | tf_op jit(solution)/shard_map/reduce_scatter | solution.py:481
  771.4 12.3 %copy-start.7 = (f32[1024,32]{0,1:T(8,128)S(1)}, f32[1024,32]{0,1:T(8,128)}, u32[]{:S(2)}) copy-start(f32[1024,32]{0,1:T(8,128)} %copy-done.6) | copy-start | bytes 393220
  771.5 12.3 %copy-start.10 = (pred[1024,32]{0,1:T(8,128)(4,1)S(1)}, pred[1024,32]{0,1:T(8,128)(4,1)}, u32[]{:S(2)}) copy-start(pred[1024,32]{0,1:T(8,128)(4,1)} %copy-done.9) | copy-start | bytes 98308
  771.5 12.3 %copy-start.17 = (f32[1024]{0:T(1024)S(1)}, f32[1024]{0:T(1024)}, u32[]{:S(2)}) copy-start(f32[1024]{0:T(1024)} %copy-done.16) | copy-start | bytes 12292
  771.5 12.3 %copy-start.19 = (f32[1024]{0:T(1024)S(1)}, f32[1024]{0:T(1024)}, u32[]{:S(2)}) copy-start(f32[1024]{0:T(1024)} %copy-done.18) | copy-start | bytes 12292
  771.5 51.0 %copy-start.1 = (bf16[1024,1024]{1,0:T(8,128)(2,1)S(1)}, bf16[1024,1024]{1,0:T(8,128)(2,1)}, u32[]{:S(2)}) copy-start(bf16[1024,1024]{1,0:T(8,128)(2,1)} %x_ref.1) | copy-start | bytes 6291460
  771.5 52.1 %copy-start.13 = (bf16[1024,32]{0,1:T(8,128)(2,1)S(1)}, bf16[1024,32]{0,1:T(8,128)(2,1)}, u32[]{:S(2)}) copy-start(bf16[1024,32]{0,1:T(8,128)(2,1)} %param.12) | copy-start | bytes 196612
  775.1 8.6 all-to-all-start
  778.5 176.7 %all-reduce.2.cloned.1.call-start = ((), (), s32[]{:S(2)}) async-start(), calls=%async_computation.3 | async-start | bytes 262144 | tf_op jit(solution)/shard_map/psum | solution.py:489
  851.0 104.2 %copy-start.8 = (bf16[1024,1024]{1,0:T(8,128)(2,1)S(1)}, bf16[1024,1024]{1,0:T(8,128)(2,1)}, u32[]{:S(2)}) copy-start(bf16[1024,1024]{1,0:T(8,128)(2,1)} %get-tuple-element.76) | copy-start | bytes 6291460
  955.2 1.3 copy-start.14
  (5 other events, 4.2 us)
Sparse Core Ops, SparseCore 0:
  13.5 221.4 all-gather.2
  297.1 145.0 reduce-scatter.4
  444.6 281.8 reduce-scatter.2
  828.0 127.2 all-reduce.1

commit v2 on v1

v2 whole, which is shorter than its diff:
```python
import functools

import jax
import jax.numpy as jnp
from jax import lax
from jax.experimental import pallas as pl
from jax.experimental.layout import Layout, with_layout_constraint
from jax.experimental.pallas import tpu as pltpu
from jax.sharding import PartitionSpec as P

LIMIT = 7.0
ALPHA = 1.702
F32 = jnp.float32
BF16 = jnp.bfloat16
PLANE = 8
DEPTH = 4
VMEM_LIMIT = 62 * 1024 * 1024


def dot(a, b, dims=((1,), (0,))):
    return lax.dot_general(a, b, (dims, ((), ())), preferred_element_type=F32)


def cost(gflops, mib):
    return pl.CostEstimate(flops=gflops * 10**9, bytes_accessed=mib * 2**20, transcendentals=0)


def place(me):
    c = me % PLANE
    core, xb, yb = c % 2, (c // 2) % 2, c // 4
    return c, me + 1 - 2 * core, me + 2 - 4 * xb, me + 4 - 8 * yb


def gather_kernel(world, cap, x_ref, dy_ref, meta_ref, bias_ref, xall, dyall, metaall, biasall, xr_hbm, qr_hbm,
                  xbuf, dybuf, xst, qst, send, recv, msend, mrecv, bsend, brecv, local, ld, st):
    me = lax.axis_index('ep')
    c, partner, xn, yn = place(me)
    base = me - c
    plane_peers = [base + (c + k) % PLANE for k in range(1, PLANE)]
    col_peers = [(me + PLANE * k) % world for k in range(1, DEPTH)]
    cx, cy, flip = xn - base, yn - base, partner - me
    cd = cx + cy - c
    half = x_ref.shape[0] // 2

    barrier = pltpu.get_barrier_semaphore()
    for peer in plane_peers + col_peers:
        pl.semaphore_signal(barrier, inc=1, device_id=(peer,), device_id_type=pl.DeviceIdType.MESH)
    pl.semaphore_wait(barrier, len(plane_peers) + len(col_peers))

    refs = ((x_ref, xall), (dy_ref, dyall))

    def hop(a, kind, arriving=False):
        if kind < 6:
            h = (0, 1, 0, 1, 0, 1)[kind]
            dev = (xn, xn, yn, yn, yn, xn)[kind]
            blk = (None, None, None, None, cx, cy)[kind]
        else:
            h, dev = kind % 2, partner
            blk = (None, cx, cy, cd)[(kind - 6) // 2]
        rows = pl.ds(h * half, half)
        source = refs[a][0].at[rows] if blk is None else refs[a][1].at[blk, rows]
        into = c if blk is None else blk
        if arriving:
            into = (cx, cx, cy, cy, cd, cd)[kind] if kind < 6 else into + flip
        return pltpu.make_async_remote_copy(
            src_ref=source, dst_ref=refs[a][1].at[into, rows],
            send_sem=send.at[a, kind], recv_sem=recv.at[a, kind],
            device_id=(dev,), device_id_type=pl.DeviceIdType.MESH)

    def small(k, peer, is_bias, arriving=False):
        if is_bias:
            return pltpu.make_async_remote_copy(
                src_ref=bias_ref, dst_ref=biasall.at[(me // PLANE + (DEPTH - k - 1 if arriving else 0)) % DEPTH],
                send_sem=bsend.at[k],
                recv_sem=brecv.at[k], device_id=(peer,), device_id_type=pl.DeviceIdType.MESH)
        return pltpu.make_async_remote_copy(
            src_ref=meta_ref.at[peer - base], dst_ref=metaall.at[(c + (PLANE - k - 1 if arriving else 0)) % PLANE],
            send_sem=msend.at[k],
            recv_sem=mrecv.at[k], device_id=(peer,), device_id_type=pl.DeviceIdType.MESH)

    smalls = [small(k, peer, False) for k, peer in enumerate(plane_peers)]
    smalls += [small(k, peer, True) for k, peer in enumerate(col_peers)]
    for cp in smalls:
        cp.start()
    for a in range(2):
        for kind in (0, 3, 1, 2):
            hop(a, kind).start()
    for a in range(2):
        for kind in (6, 7):
            hop(a, kind).start()
    bias_own = pltpu.make_async_copy(bias_ref, biasall.at[me // PLANE], local.at[0])
    bias_own.start()
    meta_own = pltpu.make_async_copy(meta_ref.at[c], metaall.at[c], local.at[1])
    meta_own.start()
    dy_own = pltpu.make_async_copy(dybuf.at[0], dyall.at[c], local.at[2])

    def block(t):
        v, f = t // 2, t % 2
        return c + (v % 2) * (cx - c) + (v // 2) * (cy - c) + f * flip

    def store(t):
        s, blk = t % 2, block(t)
        return (pltpu.make_async_copy(xst.at[s], xr_hbm.at[:, pl.ds(blk * cap, cap), :], st.at[0, s]),
                pltpu.make_async_copy(qst.at[s], qr_hbm.at[:, pl.ds(blk * cap, cap), :], st.at[1, s]))

    def arrive(a, kind, *onward):
        hop(a, kind, True).wait_recv()
        for nxt in onward:
            hop(a, nxt).start()

    def before(t):
        if t == 1:
            for n, peer in enumerate(plane_peers):
                small(n, peer, False, True).wait_recv()
            for n, peer in enumerate(col_peers):
                small(n, peer, True, True).wait_recv()
            for a in range(2):
                arrive(a, 6)
                arrive(a, 7)
        if t == 2:
            dy_own.wait()
            for a in range(2):
                arrive(a, 0, 4, 8)
                arrive(a, 3, 5, 11)
                arrive(a, 1, 9)
                arrive(a, 2, 10)
        if t in (3, 5):
            for a in range(2):
                arrive(a, 8 if t == 3 else 10)
                arrive(a, 9 if t == 3 else 11)
        if t == 6:
            for a in range(2):
                arrive(a, 4, 12)
                arrive(a, 5, 13)
        if t == 7:
            for a in range(2):
                arrive(a, 12)
                arrive(a, 13)
        s = t % 2
        blk = block(t)
        sources = (x_ref, dy_ref) if t == 0 else (xall.at[blk], dyall.at[blk])
        loads = [pltpu.make_async_copy(sources[0], xbuf.at[s], ld.at[0]),
                 pltpu.make_async_copy(sources[1], dybuf.at[s], ld.at[1])]
        for cp in loads:
            cp.start()
        for cp in loads:
            cp.wait()
        if t == 0:
            dy_own.start()
            meta_own.wait()

    slot_iota = lax.broadcasted_iota(jnp.int32, (cap, 2 * half), 0).astype(F32)

    @pl.loop(0, PLANE)
    def _(t):
        s = t % 2
        for k in range(PLANE):
            @pl.when(t == k)
            def _():
                before(k)

        @pl.when(t >= 2)
        def _():
            for cp in store(t - 2):
                cp.wait()

        blk = block(t)
        for e in range(DEPTH):
            hit = metaall[blk, e:e + 1, :] == slot_iota
            sel = jnp.where(hit, 1.0, 0.0).astype(BF16)
            w_row = jnp.sum(jnp.where(hit, metaall[blk, DEPTH + e:DEPTH + e + 1, :], 0.0), axis=1, keepdims=True)
            xst[s, e] = dot(sel, xbuf[s]).astype(BF16)
            qst[s, e] = (w_row * dot(sel, dybuf[s])).astype(BF16)
        for cp in store(t):
            cp.start()

    for t in (PLANE - 2, PLANE - 1):
        for cp in store(t):
            cp.wait()
    bias_own.wait()
    for a in range(2):
        for kind in range(14):
            hop(a, kind).wait_send()
    for cp in smalls:
        cp.wait_send()


def gather_call(world, x, dy, meta, bias, cap):
    tok, d = x.shape
    any_spec = pl.BlockSpec(memory_space=pl.ANY)
    vmem = pl.BlockSpec(memory_space=pltpu.VMEM)
    blocks = jax.ShapeDtypeStruct((PLANE, tok, d), x.dtype)
    rows = jax.ShapeDtypeStruct((DEPTH, PLANE * cap, d), BF16)
    dma = pltpu.SemaphoreType.DMA
    hops, seven, three = dma((2, 14)), dma((PLANE - 1,)), dma((DEPTH - 1,))
    return pl.pallas_call(
        functools.partial(gather_kernel, world, cap),
        in_specs=[any_spec, any_spec, vmem, vmem],
        out_specs=[any_spec, any_spec, vmem, any_spec, any_spec, any_spec],
        out_shape=[blocks, blocks, jax.ShapeDtypeStruct(meta.shape, F32),
                   jax.ShapeDtypeStruct((DEPTH,) + bias.shape, F32), rows, rows],
        scratch_shapes=[pltpu.VMEM((2, tok, d), BF16), pltpu.VMEM((2, tok, d), BF16),
                        pltpu.VMEM((2, DEPTH, cap, d), BF16), pltpu.VMEM((2, DEPTH, cap, d), BF16),
                        hops, hops, seven, seven, three, three, three, dma((2,)), dma((2, 2))],
        compiler_params=pltpu.CompilerParams(collective_id=0, has_side_effects=True, vmem_limit_bytes=60 * 2**20),
        cost_estimate=cost(100, 140),
        name="plane_gather",
    )(x, dy, meta, bias)


def swiglu_parts(h, ff):
    gate_in = h[:, :ff]
    up_in = h[:, ff:]
    g = jnp.minimum(gate_in, LIMIT)
    u1 = jnp.clip(up_in, -LIMIT, LIMIT) + 1.0
    sg = 1.0 / (1.0 + jnp.exp(-ALPHA * g))
    return gate_in, up_in, u1, sg, g * sg


def down_kernel(ff, xr_ref, qr_ref, wgu_ref, bgu_ref, act_ref, dwd_ref):
    h = dot(xr_ref[...], wgu_ref[...]) + bgu_ref[...]
    _, _, u1, _, gs = swiglu_parts(h, ff)
    act = (gs * u1).astype(BF16)
    act_ref[...] = act
    q = qr_ref[...]
    dwd = dot(act, q, ((0,), (0,)))
    dbd = jnp.broadcast_to(jnp.sum(q.astype(F32), axis=0, keepdims=True), (8, q.shape[1]))
    step = pl.program_id(1)

    @pl.when(step == 0)
    def _():
        dwd_ref[:ff] = dwd
        dwd_ref[ff:] = dbd

    @pl.when(step > 0)
    def _():
        dwd_ref[:ff] += dwd
        dwd_ref[ff:] += dbd


def down_call(x_rows, q_rows, wgu, bgu, tile):
    experts, rows, d = x_rows.shape
    ff2 = wgu.shape[2]
    ff = ff2 // 2
    per_e = lambda a, b: pl.BlockSpec((None, a, b), lambda e, s: (e, 0, 0))
    row_spec = pl.BlockSpec((None, tile, d), lambda e, s: (e, s, 0))
    return pl.pallas_call(
        functools.partial(down_kernel, ff),
        grid=(experts, rows // tile),
        in_specs=[row_spec, row_spec, per_e(d, ff2), per_e(1, ff2)],
        out_specs=[pl.BlockSpec((None, tile, ff), lambda e, s: (e, s, 0)), per_e(ff + 8, d)],
        out_shape=[jax.ShapeDtypeStruct((experts, rows, ff), BF16),
                   jax.ShapeDtypeStruct((experts, ff + 8, d), F32)],
        compiler_params=pltpu.CompilerParams(dimension_semantics=("arbitrary", "arbitrary"), vmem_limit_bytes=VMEM_LIMIT),
        cost_estimate=cost(39, 80),
        name="down_grad",
    )(x_rows, q_rows, wgu, bgu)


def up_kernel(ff, xr_ref, qr_ref, act_ref, wgu_ref, wd_ref, bgu_ref, bd_ref,
              y_ref, p_ref, dwgu_ref, dhs):
    tile = xr_ref.shape[0]
    half = tile // 2
    for i in range(2):
        rows = pl.ds(i * half, half)
        h = dot(xr_ref[rows, :], wgu_ref[...]) + bgu_ref[...]
        gate_in, up_in, u1, sg, gs = swiglu_parts(h, ff)
        da = dot(qr_ref[rows, :], wd_ref[...], ((1,), (1,)))
        pass_g = jnp.where(gate_in < LIMIT, 1.0, jnp.where(gate_in == LIMIT, 0.5, 0.0))
        up_abs = jnp.abs(up_in)
        pass_u = jnp.where(up_abs < LIMIT, 1.0, jnp.where(up_abs == LIMIT, 0.5, 0.0))
        dhs[rows, :ff] = ((da * u1) * (sg + ALPHA * gs * (1.0 - sg)) * pass_g).astype(BF16)
        dhs[rows, ff:] = (da * gs * pass_u).astype(BF16)
        p_ref[rows, :] = dot(dhs[rows, :], wgu_ref[...], ((1,), (1,))).astype(BF16)
        y_ref[rows, :] = (dot(act_ref[rows, :], wd_ref[...]) + bd_ref[...]).astype(BF16)
    dh = dhs[...]
    dwgu = dot(xr_ref[...], dh, ((0,), (0,)))
    d = dwgu.shape[0]
    dbgu = jnp.broadcast_to(jnp.sum(dh.astype(F32), axis=0, keepdims=True), (8, 2 * ff))
    step = pl.program_id(1)

    @pl.when(step == 0)
    def _():
        dwgu_ref[:d] = dwgu
        dwgu_ref[d:] = dbgu

    @pl.when(step > 0)
    def _():
        dwgu_ref[:d] += dwgu
        dwgu_ref[d:] += dbgu


def up_call(x_rows, q_rows, act, wgu, wd, bgu, bd, tile):
    experts, rows, d = x_rows.shape
    ff2 = wgu.shape[2]
    ff = ff2 // 2
    per_e = lambda a, b: pl.BlockSpec((None, a, b), lambda e, s: (e, 0, 0))
    row_spec = pl.BlockSpec((None, tile, d), lambda e, s: (e, s, 0))
    row_shape = jax.ShapeDtypeStruct((experts, rows, d), BF16)

    return pl.pallas_call(
        functools.partial(up_kernel, ff),
        grid=(experts, rows // tile),
        in_specs=[row_spec, row_spec, pl.BlockSpec((None, tile, ff), lambda e, s: (e, s, 0)),
                  per_e(d, ff2), per_e(ff, d), per_e(1, ff2), per_e(1, d)],
        out_specs=[row_spec, row_spec, per_e(d + 8, ff2)],
        out_shape=[row_shape, row_shape, jax.ShapeDtypeStruct((experts, d + 8, ff2), F32)],
        scratch_shapes=[pltpu.VMEM((tile, ff2), BF16)],
        compiler_params=pltpu.CompilerParams(dimension_semantics=("arbitrary", "arbitrary"), vmem_limit_bytes=VMEM_LIMIT),
        cost_estimate=cost(103, 140),
        name="up_grad",
    )(x_rows, q_rows, act, wgu, wd, bgu, bd)


def combine_kernel(cap, chunk, world, meta_ref, dy_hbm, y_hbm, p_hbm, gate_ref, wr_ref, hid_ref,
                   out_ref, dx_ref, fin_ref, core_in, link_in,
                   stage, ybuf, pbuf, dybuf, r_rows, r_in, dw, dw_in, dz_in, dz,
                   ysem, psem, dysem, csend, crecv, lsend, lrecv, loads,
                   rsend, rrecv, wsend, wrecv, zsend, zrecv, fsend, frecv):
    me = lax.axis_index('ep')
    c, partner, xn, yn = place(me)
    base = me - c
    core, xb, yb = c % 2, (c // 2) % 2, c // 4
    half = out_ref.shape[0] // 2
    d = out_ref.shape[1]

    barrier = pltpu.get_barrier_semaphore()
    plane_peers = [base + (c + k) % PLANE for k in range(1, PLANE)]
    col_peers = [(me + PLANE * k) % world for k in range(1, DEPTH)]
    for peer in plane_peers + col_peers:
        pl.semaphore_signal(barrier, inc=1, device_id=(peer,), device_id_type=pl.DeviceIdType.MESH)
    pl.semaphore_wait(barrier, len(plane_peers) + len(col_peers))

    def exchange(peers, source, into, at, ssem, rsem, arriving=False):
        count = len(peers) + 1
        return [pltpu.make_async_remote_copy(
            src_ref=source(peer), dst_ref=into.at[(at + (count - k - 1 if arriving else 0)) % count],
            send_sem=ssem.at[k], recv_sem=rsem.at[k],
            device_id=(peer,), device_id_type=pl.DeviceIdType.MESH) for k, peer in enumerate(peers)]

    def begin(*how):
        cps = exchange(*how)
        for cp in cps:
            cp.start()
        return how, cps

    def finish(begun):
        for cp in exchange(*begun[0], arriving=True):
            cp.wait_recv()

    def where(t):
        u, mine = t // 2, t % 2
        v, i = u // 2, u % 2
        diag = 1 - (v + 3) // 4
        side = ((v + 1) // 2) % 2
        isx, isy = diag + side * (1 - i), diag + side * i
        swap = (v // 2) * (1 - v // 3)
        h = i + swap * (1 - 2 * i)
        dest = c + isx * (2 - 4 * xb) + isy * (4 - 8 * yb) + (1 - mine) * (1 - 2 * core)
        slot = mine * (u % 6) + (1 - mine) * (6 + u % 2)
        return dest, h, mine, slot

    def fetch(t):
        dest, h, _, _ = where(t)
        b = t % 2
        return (pltpu.make_async_copy(y_hbm.at[:, pl.ds(dest * cap, cap), :], ybuf.at[b], ysem.at[b]),
                pltpu.make_async_copy(p_hbm.at[:, pl.ds(dest * cap, cap), :], pbuf.at[b], psem.at[b]),
                pltpu.make_async_copy(dy_hbm.at[dest, pl.ds(h * half, half), :], dybuf.at[b], dysem.at[b]))

    def to_core(u):
        return pltpu.make_async_remote_copy(
            src_ref=stage.at[6 + u % 2], dst_ref=core_in.at[u], send_sem=csend.at[u], recv_sem=crecv.at[u],
            device_id=(partner,), device_id_type=pl.DeviceIdType.MESH)

    def to_link(u):
        return pltpu.make_async_remote_copy(
            src_ref=stage.at[u], dst_ref=link_in.at[u], send_sem=lsend.at[u], recv_sem=lrecv.at[u],
            device_id=((xn, yn, xn, yn, xn, yn)[u],), device_id_type=pl.DeviceIdType.MESH)

    def load(src, slot, s):
        cp = pltpu.make_async_copy(src, stage.at[slot], loads.at[s])
        cp.start()
        return cp

    def add_into(slot, other):
        @pl.loop(0, half // chunk)
        def _(k):
            rows = pl.ds(pl.multiple_of(k * chunk, chunk), chunk)
            stage[slot, 0, rows, :] += stage[other, 0, rows, :]
            stage[slot, 1, rows, :] += stage[other, 1, rows, :]

    def before(t):
        u, mine = t // 2, t % 2
        if mine:
            to_core(u).wait_recv()
            load(core_in.at[u], u % 6, 0).wait()
            if u in (4, 5):
                other = 5 - u
                to_link(other).wait_recv()
                to_link(other).wait_send()
                load(link_in.at[other], other, 1).wait()
                add_into(u, other)
        elif u >= 2:
            to_core(u - 2).wait_send()

    def after(t):
        u, mine = t // 2, t % 2
        if not mine:
            to_core(u).start()
        elif u < 6:
            to_link(u).start()

    for cp in fetch(0):
        cp.start()
    slot_iota = lax.broadcasted_iota(jnp.int32, (chunk, cap), 1).astype(F32)
    lane = lax.broadcasted_iota(jnp.int32, (chunk, 128), 1)

    @pl.loop(0, 16)
    def _(t):
        dest, h, mine, slot = where(t)
        b = t % 2
        for cp in fetch(t):
            cp.wait()

        @pl.when(t < 15)
        def _():
            for cp in fetch(t + 1):
                cp.start()

        for k in range(16):
            @pl.when(t == k)
            def _():
                before(k)

        @pl.loop(0, half // chunk)
        def _(k):
            rows = pl.ds(pl.multiple_of(k * chunk, chunk), chunk)
            tokens = pl.ds(pl.multiple_of(h * half + k * chunk, chunk), chunk)
            meta = meta_ref[dest, tokens, :]
            dy = dybuf[b, rows, :].astype(F32)
            out = jnp.zeros((chunk, d), F32)
            dx = jnp.zeros((chunk, d), F32)
            r = jnp.zeros((chunk, 128), F32)
            for j in range(DEPTH):
                sel = jnp.where(meta[:, j:j + 1] == slot_iota, 1.0, 0.0).astype(BF16)
                y = dot(sel, ybuf[b, j])
                out += meta[:, DEPTH + j:DEPTH + j + 1] * y
                r = jnp.where(lane == j, jnp.sum(dy * y, axis=1, keepdims=True), r)
                dx += dot(sel, pbuf[b, j])
            r_rows[dest, :, tokens] = jnp.transpose(r)[:8, :]

            @pl.when(mine == 0)
            def _():
                stage[slot, 0, rows, :] = out
                stage[slot, 1, rows, :] = dx

            @pl.when(mine == 1)
            def _():
                stage[slot, 0, rows, :] += out
                stage[slot, 1, rows, :] += dx

        for k in range(16):
            @pl.when(t == k)
            def _():
                after(k)

    r_cps = begin(plane_peers, lambda peer: r_rows.at[peer - base], r_in, c, rsend, rrecv)

    for slot, (first, second) in ((0, (2, 5)), (1, (4, 3))):
        for n in (first, second):
            to_link(n).wait_recv()
            to_link(n).wait_send()
            load(link_in.at[n], n, 1).wait()
            add_into(slot, n)
        out_ref[pl.ds(slot * half, half), :] = stage[slot, 0].astype(BF16)

    finish(r_cps)
    r_in[c] = r_rows[c]
    flat = (8 * PLANE, 2 * half)
    gate = gate_ref[...].reshape(flat)
    r_all = r_in[...].reshape(flat)
    mean = jnp.sum(gate * r_all, axis=0, keepdims=True)
    dl = (gate * (r_all - mean)).astype(BF16)
    dw[:, :, :d] = dot(dl, hid_ref[...]).reshape(PLANE, 8, d)
    dbias = jnp.sum(dl.astype(F32), axis=1, keepdims=True)
    dw[:, :, d:] = jnp.broadcast_to(dbias, (8 * PLANE, 128)).reshape(PLANE, 8, 128)
    w_cps = begin(plane_peers, lambda peer: dw.at[peer - base], dw_in, c, wsend, wrecv)
    for slot in range(2):
        part = dot(dl[:, slot * half:(slot + 1) * half], wr_ref[...], ((0,), (0,)))
        dx_ref[pl.ds(slot * half, half), :] = (stage[slot, 1] + part).astype(BF16)
    finish(w_cps)
    dw_in[c] = dw[c]
    dz[...] = jnp.sum(dw_in[...], axis=0)
    z_cps = begin(col_peers, lambda peer: dz, dz_in, me // PLANE, zsend, zrecv)
    finish(z_cps)
    dz_in[me // PLANE] = dz[...]
    fin_ref[c] = (dz_in[0] + dz_in[1]) + (dz_in[2] + dz_in[3])
    f_cps = begin(plane_peers, lambda peer: fin_ref.at[c], fin_ref, c, fsend, frecv)
    finish(f_cps)
    to_core(6).wait_send()
    to_core(7).wait_send()
    for cp in r_cps[1] + w_cps[1] + z_cps[1] + f_cps[1]:
        cp.wait_send()


def combine_call(world, meta_t, dy_all, y_rows, p_rows, gate, w_rows, hidden, cap):
    srcs, tok, d = dy_all.shape
    half = tok // 2
    any_spec = pl.BlockSpec(memory_space=pl.ANY)
    vmem = pl.BlockSpec(memory_space=pltpu.VMEM)
    two, three, six, seven, eight = (pltpu.SemaphoreType.DMA((n,)) for n in (2, 3, 6, 7, 8))
    chunk = min(128, half)
    wide = d + 128
    return pl.pallas_call(
        functools.partial(combine_kernel, cap, chunk, world),
        in_specs=[vmem, any_spec, any_spec, any_spec, vmem, vmem, vmem],
        out_specs=[vmem, vmem, vmem, any_spec, any_spec],
        out_shape=[jax.ShapeDtypeStruct((tok, d), BF16), jax.ShapeDtypeStruct((tok, d), BF16),
                   jax.ShapeDtypeStruct((PLANE, 8, wide), F32),
                   jax.ShapeDtypeStruct((8, 2, half, d), F32), jax.ShapeDtypeStruct((6, 2, half, d), F32)],
        scratch_shapes=[pltpu.VMEM((8, 2, half, d), F32),
                        pltpu.VMEM((2, DEPTH, cap, d), BF16), pltpu.VMEM((2, DEPTH, cap, d), BF16),
                        pltpu.VMEM((2, half, d), BF16),
                        pltpu.VMEM((PLANE, 8, tok), F32), pltpu.VMEM((PLANE, 8, tok), F32),
                        pltpu.VMEM((PLANE, 8, wide), F32), pltpu.VMEM((PLANE, 8, wide), F32),
                        pltpu.VMEM((DEPTH, 8, wide), F32), pltpu.VMEM((8, wide), F32),
                        two, two, two, eight, eight, six, six, two,
                        seven, seven, seven, seven, three, three, seven, seven],
        compiler_params=pltpu.CompilerParams(collective_id=1, has_side_effects=True, vmem_limit_bytes=67043328),
        cost_estimate=cost(300, 300),
        name="combine_scatter",
    )(meta_t, dy_all, y_rows, p_rows, gate, w_rows, hidden)


def interleave_kernel(ff, w_ref, out_ref, bias_ref):
    ff2 = 2 * ff
    src = lax.broadcasted_iota(jnp.int32, (ff2, ff2), 0)
    dst = lax.broadcasted_iota(jnp.int32, (ff2, ff2), 1)
    perm = jnp.where(src == dst // 2 + ff * (dst % 2), 1.0, 0.0).astype(BF16)

    def move(v):
        a = v.astype(BF16)
        rest = v - a.astype(F32)
        b = rest.astype(BF16)
        return dot(a, perm) + (dot(b, perm) + dot((rest - b.astype(F32)).astype(BF16), perm))

    d = out_ref.shape[0]
    out_ref[...] = move(w_ref[:d, :])
    bias_ref[...] = move(w_ref[d:, :])


def interleave_call(w, ff):
    rows, ff2 = w.shape
    return pl.pallas_call(
        functools.partial(interleave_kernel, ff),
        out_shape=[jax.ShapeDtypeStruct((rows - 8, ff2), F32), jax.ShapeDtypeStruct((8, ff2), F32)],
        compiler_params=pltpu.CompilerParams(vmem_limit_bytes=48 * 2**20),
        name="interleave",
    )(w)


def solution(mesh):
    world = mesh.shape['ep']
    plane_groups = [[PLANE * z + c for c in range(PLANE)] for z in range(DEPTH)]
    col_groups = [[PLANE * z + c for z in range(DEPTH)] for c in range(PLANE)]

    def local_block(hidden, grad_out, w_router, b_router, expert_ids, slot_ids, w_gate_up, b_gate_up, w_down, b_down):
        tok, d = hidden.shape
        top_k = expert_ids.shape[1]
        experts = w_router.shape[1]
        ff = w_down.shape[1]
        cap = (3 * tok * top_k + 2 * experts - 1) // (2 * experts)

        ids = jnp.arange(experts, dtype=jnp.int32)
        match = expert_ids[:, :, None] == ids
        chosen = jnp.any(match, axis=1)
        slot = jnp.max(jnp.where(match, slot_ids[:, :, None], -1), axis=1)
        logits = jnp.dot(hidden, w_router, preferred_element_type=F32) + b_router
        peak = jnp.max(jnp.where(chosen, logits, -jnp.inf), axis=1, keepdims=True)
        expd = jnp.where(chosen, jnp.exp(jnp.where(chosen, logits, peak) - peak), 0.0)
        gate = expd / jnp.sum(expd, axis=1, keepdims=True)
        meta = jnp.concatenate([slot.astype(F32).reshape(tok, DEPTH, PLANE), gate.reshape(tok, DEPTH, PLANE)], axis=1)

        col = jnp.arange(2 * ff, dtype=jnp.int32)
        perm = (col[:, None] == jnp.where(col < ff, 2 * col, 2 * (col - ff) + 1)[None, :]).astype(BF16)
        wgu = jnp.dot(w_gate_up[0], perm, preferred_element_type=F32).astype(BF16)
        bgu = b_gate_up.reshape(ff, 2).T.reshape(1, 2 * ff)
        wgu = with_layout_constraint(wgu[None], Layout((0, 1, 2)))
        wgu_all = lax.all_gather(wgu, 'ep', axis_index_groups=col_groups, tiled=True)
        wd_all = lax.all_gather(w_down[0], 'ep', axis_index_groups=col_groups)
        bias = jnp.concatenate([bgu, b_down, jnp.zeros((6, d), F32)], axis=0)
        _, dy_all, meta_r, b_cat, x_rows, q_rows = gather_call(world, hidden, grad_out, meta.transpose(2, 1, 0), bias, cap)
        meta_t = meta_r.transpose(0, 2, 1)
        bgu_all, bd_all = b_cat[:, :1], b_cat[:, 1:2]

        act, dwd = down_call(x_rows, q_rows, wgu_all, bgu_all, 2 * cap)
        y_rows, p_rows, dwgu = up_call(x_rows, q_rows, act, wgu_all, wd_all, bgu_all, bd_all, 2 * cap)
        gate_rows = jnp.pad(gate.T.reshape(DEPTH, PLANE, tok).transpose(1, 0, 2), ((0, 0), (0, 4), (0, 0)))
        w_rows = jnp.pad(w_router.T.reshape(DEPTH, PLANE, d).transpose(1, 0, 2), ((0, 0), (0, 4), (0, 0)))
        block_out, grad_hidden, router, _, _ = combine_call(
            world, meta_t, dy_all, y_rows, p_rows, gate_rows, w_rows.reshape(8 * PLANE, d), hidden, cap)

        scatter = functools.partial(lax.psum_scatter, axis_name='ep', scatter_dimension=0, tiled=True)
        grad_wd = scatter(dwd, axis_index_groups=col_groups)
        grad_wgu = scatter(dwgu, axis_index_groups=col_groups)

        grad_w_router = router[:, :DEPTH, :d].transpose(2, 1, 0).reshape(d, experts)
        grad_b_router = router[:, :DEPTH, d].T.reshape(experts)
        grad_w_gate_up, grad_b_gate_up = interleave_call(grad_wgu[0], ff)
        return (block_out, grad_hidden, grad_w_router, grad_b_router, grad_w_gate_up[None],
                grad_b_gate_up[:1], grad_wd[:, :ff], grad_wd[:, ff])

    tok_spec = P('ep', None)
    in_specs = (tok_spec, tok_spec, P(None, None), P(None), tok_spec, tok_spec, P('ep', None, None), P('ep', None), P('ep', None, None), P('ep', None))
    out_specs = (tok_spec, tok_spec, P(None, None), P(None), P('ep', None, None), P('ep', None), P('ep', None, None), P('ep', None))
    return jax.shard_map(local_block, mesh=mesh, in_specs=in_specs, out_specs=out_specs, check_vma=False)
```

time: 965 us -> 764 us (0.79)
  waiting for transfers between devices: 102 us -> 3.79 us
  blocking collectives: 38.4 us -> 0 us
  local copies, waits for them, and re-layouts: 59.9 us -> 22.2 us
  Pallas kernels: 729 us -> 713 us
    psum x1 -> x0, waiting for transfers between devices: 97 us -> none  [local_block(): lax.psum(lax.dot_general(hidden, logit_grad, (((0,), (0,)), ((), ())), pr...]
    psum x1 -> x0, blocking collectives: 38.4 us -> none  [local_block(): grad_b_router = lax.psum(jnp.sum(logit_grad.astype(F32), axis=0), 'ep')]
    pallas_call x4, Pallas kernels: 675 us -> 659 us  [the longest x1 348 us: combine_call(): pl.pallas_call(functools.partial(combine_kernel, cap, chunk, world), in_s...]
    slice x5 -> x4, local copies, waits for them, and re-layouts: 17.4 us -> 3.08 us  [the longest x1 1.62 us: local_block(): bgu_all, bd_all = (b_cat[:, :1], b_cat[:, 1:2])]
    unnamed x53 -> x44, local copies, waits for them, and re-layouts: 17.7 us -> 7.42 us
    another operation x4 -> x0, local copies, waits for them, and re-layouts: 10.2 us -> none  [the longest x2 10 us: local_block(): jnp.stack([grad_wgu[0, :d, :ff], grad_wgu[0, :d, ff:]], axis=-1)]
  transfers between devices with their start and end apart: 5 -> 4, of which waited for: 2 -> 1; matrix products, arithmetic and copies ran while one was open for 5% -> 2% of each run, Pallas kernels for 70% -> 92%
where the time goes in v2:
time: 764 us; the launch traced here: 763 us
  Pallas kernels  713 us (93%)
  local copies, waits for them, and re-layouts  22.2 us (3%)
  between operations  14 us (2%)
    pallas_call x1, Pallas kernels, combine_call(): pl.pallas_call(functools.partial(combine_kernel, cap, chunk, world), in_s...  348 us
    pallas_call x1, Pallas kernels, gather_call(): pl.pallas_call(functools.partial(gather_kernel, world, cap), in_specs=[an...  169 us
    pallas_call x1, Pallas kernels, up_call(): pl.pallas_call(functools.partial(up_kernel, ff), grid=(experts, rows // t...  134 us
    pallas_call x1, Pallas kernels, down_call(): pl.pallas_call(functools.partial(down_kernel, ff), grid=(experts, rows //...  53.8 us
  transfers between devices with their start and end apart: 4, of which 1 were waited for; matrix products, arithmetic and copies ran while one was open for 2% of the time, Pallas kernels for 92%

profile of v2, /device:TPU:0, one launch (start us, length us, event | category | flops | bytes accessed | tf_op | source)
XLA Modules:
  0.0 762.7 jit_solution(1126721015053256900)
XLA Ops:
  7.3 5.5 convert_bitcast_fusion
  12.8 0.7 all-gather.5.cloned.1.call-update
  13.9 0.7 select_reduce_fusion.1
  17.8 0.8 maximum_bitcast_fusion.meta_ref
  18.7 0.7 maximum_maximum_fusion.bias_ref
  19.4 168.6 %plane_gather.1 = (bf16[8,1024,1024]{2,1,0:T(8,128)(2,1)}, bf16[8,1024,1024]{2,1,0:T(8,128)(2,1)}, f32[8,8,1024]{2,1,0:T(8,128)}, f32[4,8,1024]{2,1,0:T(8,128)},...) custom-call(bf16[1024,1024]{1,0:T(8,128)(2,1)} %hid_ref.1, bf16[1024,1024]{1,0:T(8,128)(2,1)} %dy_ref.1, ...), custom_call_target="tpu_custom_call" | custom-call | flops 99999997952 | bytes 146800640 | tf_op jit(solution)/shard_map/plane_gather/pallas_call | solution.py:196
  187.9 1.6 fusion.15
  189.6 53.8 %down_grad.1 = (bf16[4,3072,512]{2,1,0:T(8,128)(2,1)}, f32[4,520,1024]{2,1,0:T(8,128)}) custom-call(bf16[4,3072,1024]{2,1,0:T(8,128)(2,1)} %get-tuple-element.25.xr_ref, bf16[4,3072,1024]{2,1,0:T(8,128)(2,1)} %get-tuple-element.26.qr_ref, bf16[4,1024,1024]{2,1,0:T(8,128)(2,1)} %all-gather.3.cloned.1.call-done.wgu_ref, f32[4,1,1024]{2,1,0:T(1,128)} %get-tuple-element.39.bgu_ref), custom_call_target="tpu_custom_call" | custom-call | flops 38999998464 | bytes 83886080 | tf_op jit(solution)/shard_map/down_grad/pallas_call | solution.py:247
  243.6 3.0 all-gather.5.cloned.1.call-done.wd_ref
  246.7 134.1 %up_grad.1 = (bf16[4,3072,1024]{2,1,0:T(8,128)(2,1)}, bf16[4,3072,1024]{2,1,0:T(8,128)(2,1)}, f32[4,1032,1024]{2,1,0:T(8,128)}) custom-call(bf16[4,3072,1024]{2,1,0:T(8,128)(2,1)} %get-tuple-element.25.xr_ref, bf16[4,3072,1024]{2,1,0:T(8,128)(2,1)} %get-tuple-element.26.qr_ref, bf16[4,3072,512]{2,1,0:T(8,128)(2,1)} %get-tuple-element.28.act_ref, ...), custom_call_target="tpu_custom_call" | custom-call | flops 102999998464 | bytes 146800640 | tf_op jit(solution)/shard_map/up_grad/pallas_call | solution.py:301
  380.9 0.9 copy-done.8
  381.7 2.7 copy.47
  384.6 0.7 pad.8.gate_ref
  385.3 0.7 pad_bitcast_fusion.wr_ref
  386.0 348.1 %combine_scatter.1 = (bf16[1024,1024]{1,0:T(8,128)(2,1)}, bf16[1024,1024]{1,0:T(8,128)(2,1)}, f32[8,8,1152]{2,1,0:T(8,128)}, f32[8,2,512,1024]{3,2,1,0:T(8,128)}, f32[6,2,512,1024]{3,2,1,0:T(8,128)}) custom-call(f32[8,1024,8]{2,1,0:T(8,128)} %bitcast.62, bf16[8,1024,1024]{2,1,0:T(8,128)(2,1)} %get-tuple-element.24.dy_hbm, ...), custom_call_target="tpu_custom_call" | custom-call | flops 299999985664 | bytes 314572800 | tf_op jit(solution)/shard_map/combine_scatter/pallas_call | solution.py:514
  734.1 0.8 slice.24
  734.9 1.0 slice_bitcast_fusion
  735.9 0.7 copy.56
  737.3 3.3 slice.28
  740.6 1.4 slice_bitcast_fusion.1
  742.0 2.2 copy-done
  744.2 8.7 %interleave.1 = (f32[1024,1024]{1,0:T(8,128)}, f32[8,1024]{1,0:T(8,128)S(1)}) custom-call(f32[1032,1024]{1,0:T(8,128)S(1)} %bitcast.61), custom_call_target="tpu_custom_call" | custom-call | tf_op jit(solution)/shard_map/interleave/pallas_call | solution.py:554
  753.5 1.3 copy.61
  754.8 1.3 copy.62
  (69 shorter events, 5.4 us)
Async XLA Ops:
  7.2 182.4 %all-gather.3.cloned.1.call-start = ((), (), s32[]{:S(2)}) async-start(), calls=%async_computation.2 | async-start | bytes 10485760 | tf_op jit(solution)/shard_map/all_gather | solution.py:589
  7.2 6.5 copy-start.11
  7.2 6.7 copy-start.3
  7.2 6.7 copy-start.9
  7.3 6.7 copy-start.19
  12.8 3.3 copy-start.16
  12.8 4.1 copy-start.17
  12.8 5.9 copy-start.18
  12.8 233.9 %all-gather.5.cloned.1.call-start = ((), (), s32[]{:S(2)}) async-start(), calls=%async_computation.3 | async-start | bytes 5242880 | tf_op jit(solution)/shard_map/all_gather | solution.py:590
  13.5 723.8 %reduce-scatter.5.cloned.1.call-start = ((), (), s32[]{:S(2)}) async-start(), calls=%async_computation.5 | async-start | bytes 10649600 | tf_op jit(solution)/shard_map/reduce_scatter | solution.py:604
  13.9 1.5 copy-start.6
  14.7 0.7 copy-start.1
  14.7 1.5 copy-start.12
  15.4 0.6 copy-start.14
  243.4 498.6 %reduce-scatter.3.cloned.1.call-start = ((), (), s32[]{:S(2)}) async-start(), calls=%async_computation.4 | async-start | bytes 21135360 | tf_op jit(solution)/shard_map/reduce_scatter | solution.py:605
  380.8 0.9 copy-start.8
  380.8 3.6 copy-start.2
  380.8 3.6 copy-start.7
  380.8 3.6 copy-start.13
  380.8 3.6 copy-start.15
  380.9 4.4 copy-start.10
  737.3 16.2 %copy-start.5 = (bf16[1024,1024]{1,0:T(8,128)(2,1)S(1)}, bf16[1024,1024]{1,0:T(8,128)(2,1)}, u32[]{:S(2)}) copy-start(bf16[1024,1024]{1,0:T(8,128)(2,1)} %get-tuple-element.50) | copy-start | bytes 6291460
  742.0 2.2 copy-start
  744.2 10.6 %copy-start.4 = (bf16[1024,1024]{1,0:T(8,128)(2,1)S(1)}, bf16[1024,1024]{1,0:T(8,128)(2,1)}, u32[]{:S(2)}) copy-start(bf16[1024,1024]{1,0:T(8,128)(2,1)} %get-tuple-element.51) | copy-start | bytes 6291460
Sparse Core Ops, SparseCore 0:
  12.9 153.0 all-gather.2
  167.6 79.0 all-gather.4
  249.0 144.9 reduce-scatter.4
  396.3 281.8 reduce-scatter.2
